TPU v7x, 16 devices: a 4x2x1 block of a 4x4x8 slice. The times are simulated.
16 devices in a mesh: rep: 4 (over y, z, core), dp: 4 (over x).
Axes of the slice: x: 4, y: 2, z: 1, core: 2. Of those that a mesh axis runs over, the one named last changes fastest.
The devices are a block of a 4x4x8 slice.
Arguments:
- x: bfloat16 [16, 4096, 896], P(('rep', 'dp')), parts along dimension 0
- dy: bfloat16 [16, 4096, 896], P(('rep', 'dp')), parts along dimension 0
- w_gate: bfloat16 [2, 896, 2560], P(None, 'dp')
- w_up: bfloat16 [2, 896, 2560], P(None, 'dp')
- w_down: bfloat16 [2, 2560, 896], P(None, 'dp')
- m_w_gate: float32 [2, 896, 2560], P(None, 'dp')
- m_w_up: float32 [2, 896, 2560], P(None, 'dp')
- m_w_down: float32 [2, 2560, 896], P(None, 'dp')
- v_w_gate: float32 [2, 896, 2560], P(None, 'dp')
- v_w_up: float32 [2, 896, 2560], P(None, 'dp')
- v_w_down: float32 [2, 2560, 896], P(None, 'dp')
Outputs:
- output 1: bfloat16 [8, 896, 2560], P('rep', 'dp'), parts along dimension 0
- output 2: bfloat16 [8, 896, 2560], P('rep', 'dp'), parts along dimension 0
- output 3: bfloat16 [8, 2560, 896], P('rep', 'dp'), parts along dimension 0
- output 4: float32 [8, 896, 2560], P('rep', 'dp'), parts along dimension 0
- output 5: float32 [8, 896, 2560], P('rep', 'dp'), parts along dimension 0
- output 6: float32 [8, 2560, 896], P('rep', 'dp'), parts along dimension 0
- output 7: float32 [8, 896, 2560], P('rep', 'dp'), parts along dimension 0
- output 8: float32 [8, 896, 2560], P('rep', 'dp'), parts along dimension 0
- output 9: float32 [8, 2560, 896], P('rep', 'dp'), parts along dimension 0
There are 4 independent parts. A program takes and returns all parts, laid end to end along the dimension named above; an argument that names none is the same for every part.
All inputs are finite; a program needn't handle non-finite values.
Results may differ from a plain program's by a relative error of at most 0.022.
Values are sent between devices in bfloat16 or wider.
A program may use at most 768 MiB of HBM per device.

v0:
```python
import jax
import jax.numpy as jnp
from jax import lax
from jax.sharding import PartitionSpec as P

NAMES = ("w_gate", "w_up", "w_down")


def matmul(a, w):
    return jnp.dot(a, w, preferred_element_type=jnp.float32).astype(jnp.bfloat16)


def normed(h):
    wide = h.astype(jnp.float32)
    scale = lax.rsqrt(jnp.mean(wide**2, -1, keepdims=True) + 1e-6)
    return (wide * scale).astype(jnp.bfloat16)


def layer(h, w):
    a = normed(h)
    gate = jnp.dot(a, w["w_gate"], preferred_element_type=jnp.float32)
    up = jnp.dot(a, w["w_up"], preferred_element_type=jnp.float32)
    return h + matmul((jax.nn.silu(gate) * up).astype(jnp.bfloat16), w["w_down"])


def adamw(w, m, v, g):
    m = 0.9 * m + 0.1 * g
    v = 0.95 * v + 0.05 * g * g
    step = m * lax.rsqrt(v + 1e-8) + 0.1 * w
    return (w - 0.02 * step).astype(jnp.bfloat16), m, v


def clipped(gradients, sum_of_squares, count):
    factor = jnp.minimum(1.0, 0.5 * lax.rsqrt(sum_of_squares / count + 1e-30))
    return [g * factor for g in gradients]


def solution(mesh):
    def fetched(weights, number):
        return {name: lax.all_gather(w[number], "dp", axis=0, tiled=True) for name, w in zip(NAMES, weights, strict=True)}

    def step(x, dy, *arrays):
        weights, m, v = (arrays[i : i + 3] for i in (0, 3, 6))
        layers = weights[0].shape[0]
        h, kept = x[0], []
        for number in range(layers):
            kept.append(h)
            h = layer(h, fetched(weights, number))
        by_h, mine = dy[0], [None] * layers
        for number in reversed(range(layers)):
            _, back = jax.vjp(lambda w, h: layer(h, w), fetched(weights, number), kept[number])
            by_w, by_h = back(by_h)
            mine[number] = [lax.psum_scatter(by_w[name], "dp", scatter_dimension=0, tiled=True) for name in NAMES]
        gradients = [jnp.stack([mine[number][i] for number in range(layers)]).astype(jnp.float32) for i in range(3)]
        squares = lax.psum(sum(jnp.sum(g * g) for g in gradients), "dp")
        gradients = clipped(gradients, squares, lax.psum(1, "dp") * sum(g.size for g in gradients))
        new = [adamw(w.astype(jnp.float32), m, v, g) for w, m, v, g in zip(weights, m, v, gradients, strict=True)]
        return tuple(one[which] for which in range(3) for one in new)

    states, cut = P(("rep", "dp"), None, None), P(None, "dp", None)
    return jax.shard_map(
        step,
        mesh=mesh,
        in_specs=(states, states) + (cut,) * 9,
        out_specs=(P("rep", "dp", None),) * 9,
        check_vma=False,
    )
```

profile of v0, /device:TPU:112, one launch (start us, length us, event | category | flops | bytes accessed | tf_op | source)
XLA Modules:
  0.0 805.4 jit_solution(6017654960096533541)
XLA Ops:
  17.6 10.7 %copy.20 = bf16[1,4096,896]{1,2,0:T(8,128)(2,1)} copy(bf16[1,4096,896]{2,1,0:T(8,128)(2,1)} %param.11) | data formatting | bytes 14680064 | tf_op args[0]
  28.3 4.6 fusion.15
  32.9 10.8 %copy.21 = bf16[1,4096,896]{1,2,0:T(8,128)(2,1)} copy(bf16[1,4096,896]{2,1,0:T(8,128)(2,1)} %param.12) | data formatting | bytes 14680064 | tf_op args[1]
  43.7 17.2 %all-gather.13.cloned.1.call-done = bf16[1,896,2560]{2,1,0:T(8,128)(2,1)} async-done(((bf16[1,224,2560]{2,1,0:T(8,128)(2,1)}), bf16[1,896,2560]{2,1,0:T(8,128)(2,1)}) %all-gather.13.cloned.1.call-update) | async-done | bytes 4587536 | tf_op jit(solution)/shard_map/all_gather | solution.py:40
  60.9 29.4 %fusion.47 = f32[4096,2560]{1,0:T(8,128)} fusion(bf16[1,4096,896]{1,2,0:T(8,128)(2,1)} %copy.20, f32[4096]{0:T(1024)S(1)} %add_rsqrt_fusion, bf16[1,896,2560]{2,1,0:T(8,128)(2,1)} %all-gather.13.cloned.1.call-done), kind=kOutput, calls=%fused_computation.72 | convolution fusion | flops 18801491968 | bytes 53886976 | tf_op jit(solution)/shard_map/dot_general | solution.py:21
  90.3 20.4 %all-gather.15.cloned.1.call-done = bf16[1,896,2560]{2,1,0:T(8,128)(2,1)} async-done(((bf16[1,224,2560]{2,1,0:T(8,128)(2,1)}), bf16[1,896,2560]{2,1,0:T(8,128)(2,1)}) %all-gather.15.cloned.1.call-update) | async-done | bytes 4587536 | tf_op jit(solution)/shard_map/all_gather | solution.py:40
  110.8 49.8 %multiply_convert_fusion.1 = (bf16[4096,2560]{1,0:T(8,128)(2,1)}, f32[4096,2560]{1,0:T(8,128)}) fusion(f32[4096,2560]{1,0:T(8,128)} %fusion.47, bf16[1,896,2560]{2,1,0:T(8,128)(2,1)} %all-gather.15.cloned.1.call-done, bf16[1,4096,896]{1,2,0:T(8,128)(2,1)} %copy.20, f32[4096]{0:T(1024)S(1)} %add_rsqrt_fusion), kind=kOutput, calls=%fused_computation.17 | convolution fusion | flops 18864406528 | bytes 116801536 | tf_op jit(solution)/shard_map/dot_general | solution.py:22
  160.6 26.8 %fusion.19 = (f32[4096]{0:T(1024)S(1)}, bf16[4096,896]{0,1:T(8,128)(2,1)}) fusion(bf16[4096,2560]{1,0:T(8,128)(2,1)} %get-tuple-element.24, bf16[1,2560,896]{2,1,0:T(8,128)(2,1)} %all-gather.17.cloned.1.call-done, bf16[1,4096,896]{1,2,0:T(8,128)(2,1)} %copy.20), kind=kOutput, calls=%fused_computation.37 | convolution fusion | flops 18808827904 | bytes 40255488 | tf_op jit(solution)/shard_map/dot_general | solution.py:10
  188.1 22.3 %all-gather.23.cloned.1.call-done = bf16[1,896,2560]{2,1,0:T(8,128)(2,1)} async-done(((bf16[1,224,2560]{2,1,0:T(8,128)(2,1)}), bf16[1,896,2560]{2,1,0:T(8,128)(2,1)}) %all-gather.23.cloned.1.call-update) | async-done | bytes 4587536 | tf_op jit(solution)/shard_map/all_gather | solution.py:40
  210.4 29.6 %fusion.39 = f32[4096,2560]{1,0:T(8,128)} fusion(bf16[4096,896]{0,1:T(8,128)(2,1)} %get-tuple-element.27, f32[4096]{0:T(1024)S(1)} %fusion.77, bf16[1,896,2560]{2,1,0:T(8,128)(2,1)} %all-gather.23.cloned.1.call-done), kind=kOutput, calls=%fused_computation.69 | convolution fusion | flops 18801491968 | bytes 53886976 | tf_op jit(solution)/shard_map/jvp()/dot_general | solution.py:22
  240.0 20.1 %all-gather.21.cloned.1.call-done = bf16[1,2560,896]{2,1,0:T(8,128)(2,1)} async-done(((bf16[1,640,896]{2,1,0:T(8,128)(2,1)}), bf16[1,2560,896]{2,1,0:T(8,128)(2,1)}) %all-gather.21.cloned.1.call-update) | async-done | bytes 4587536 | tf_op jit(solution)/shard_map/all_gather | solution.py:40
  260.1 28.4 %convolution_convert_fusion.1 = bf16[4096,2560]{1,0:T(8,128)(2,1)} fusion(bf16[1,4096,896]{2,1,0:T(8,128)(2,1)} %param.12, bf16[1,2560,896]{2,1,0:T(8,128)(2,1)} %all-gather.21.cloned.1.call-done), kind=kOutput, calls=%fused_computation.27 | convolution fusion | flops 18800967680 | bytes 32899072 | tf_op jit(solution)/shard_map/transpose(jvp())/dot_general | solution.py:10
  288.5 21.3 %all-gather.19.cloned.1.call-done = bf16[1,896,2560]{2,1,0:T(8,128)(2,1)} async-done(((bf16[1,224,2560]{2,1,0:T(8,128)(2,1)}), bf16[1,896,2560]{2,1,0:T(8,128)(2,1)}) %all-gather.19.cloned.1.call-update) | async-done | bytes 4587536 | tf_op jit(solution)/shard_map/all_gather | solution.py:40
  309.8 58.3 %fusion.2 = (bf16[4096,2560]{1,0:T(8,128)(2,1)}, f32[4096,2560]{1,0:T(8,128)}) fusion(f32[4096,2560]{1,0:T(8,128)} %fusion.39, bf16[4096,2560]{1,0:T(8,128)(2,1)} %convolution_convert_fusion.1, bf16[1,896,2560]{2,1,0:T(8,128)(2,1)} %all-gather.19.cloned.1.call-done, bf16[4096,896]{0,1:T(8,128)(2,1)} %get-tuple-element.27, f32[4096]{0:T(1024)S(1)} %fusion.77), kind=kOutput, calls=%fused_computation.8 | convolution fusion | flops 18927321088 | bytes 137773056 | tf_op jit(solution)/shard_map/jvp()/dot_general | solution.py:21
  368.1 23.5 %fusion.70 = bf16[4096,896]{0,1:T(8,128)(2,1)} fusion(bf16[4096,2560]{1,0:T(8,128)(2,1)} %get-tuple-element.28, bf16[1,896,2560]{2,1,0:T(8,128)(2,1)S(1)} %copy-done.11), kind=kOutput, calls=%fused_computation.94 | convolution fusion | flops 18790481920 | bytes 32899072 | tf_op jit(solution)/shard_map/transpose(jvp())/dot_general | solution.py:21
  391.7 38.3 %fusion.21 = (f32[4096]{0:T(1024)S(1)}, bf16[4096,896]{0,1:T(8,128)(2,1)}) fusion(bf16[4096,896]{0,1:T(8,128)(2,1)} %get-tuple-element.27, bf16[4096,896]{0,1:T(8,128)(2,1)} %fusion.70, bf16[1,896,2560]{2,1,0:T(8,128)(2,1)} %all-gather.23.cloned.1.call-done, bf16[4096,2560]{1,0:T(8,128)(2,1)} %convolution_convert_fusion.1, f32[4096,2560]{1,0:T(8,128)} %get-tuple-element.29), kind=kOutput, calls=%fused_computation.39 | convolution fusion | flops 18875412480 | bytes 89538560 | tf_op jit(solution)/shard_map/transpose(jvp())/dot_general | solution.py:22
  430.0 9.8 %fusion.22 = bf16[4096,896]{0,1:T(8,128)(2,1)S(1)} fusion(bf16[4096,896]{0,1:T(8,128)(2,1)} %get-tuple-element.27, bf16[4096,896]{0,1:T(8,128)(2,1)} %get-tuple-element.31, bf16[1,4096,896]{1,2,0:T(8,128)(2,1)} %copy.21, f32[4096]{0:T(1024)S(1)} %multiply_multiply_fusion.3, f32[4096]{0:T(1024)S(1)} %fusion.77), kind=kLoop, calls=%fused_computation.40 | loop fusion | flops 25690112 | bytes 29392896 | tf_op jit(solution)/shard_map/transpose(jvp())/add_any | solution.py:14
  442.8 26.4 %convolution_convert_fusion.2 = bf16[2560,896]{1,0:T(8,128)(2,1)} fusion(bf16[4096,2560]{1,0:T(8,128)(2,1)} %get-tuple-element.24, bf16[4096,896]{0,1:T(8,128)(2,1)S(1)} %fusion.22), kind=kOutput, calls=%fused_computation.67 | convolution fusion | flops 18792775680 | bytes 32899072 | tf_op jit(solution)/shard_map/transpose(jvp())/dot_general | solution.py:10
  469.8 35.9 %fusion.29 = bf16[2560,896]{1,0:T(8,128)(2,1)} fusion(bf16[1,4096,896]{2,1,0:T(8,128)(2,1)} %param.12, f32[4096,2560]{1,0:T(8,128)} %fusion.39, f32[4096,2560]{1,0:T(8,128)} %get-tuple-element.29), kind=kOutput, calls=%fused_computation.63 | convolution fusion | flops 18855690240 | bytes 95813632 | tf_op jit(solution)/shard_map/transpose(jvp())/dot_general | solution.py:10
  505.9 27.8 %convolution_convert_fusion = bf16[4096,2560]{1,0:T(8,128)(2,1)} fusion(bf16[4096,896]{0,1:T(8,128)(2,1)} %copy-done.3, bf16[1,2560,896]{2,1,0:T(8,128)(2,1)} %all-gather.17.cloned.1.call-done), kind=kOutput, calls=%fused_computation.26 | convolution fusion | flops 18800967680 | bytes 32899072 | tf_op jit(solution)/shard_map/transpose(jvp())/dot_general | solution.py:10
  533.6 33.9 %fusion.36 = bf16[896,2560]{1,0:T(8,128)(2,1)} fusion(bf16[4096,2560]{1,0:T(8,128)(2,1)} %convolution_convert_fusion, f32[4096,2560]{1,0:T(8,128)} %fusion.47, bf16[1,4096,896]{1,2,0:T(8,128)(2,1)} %copy.20, f32[4096]{0:T(1024)S(1)} %copy-done.10), kind=kOutput, calls=%fused_computation.66 | convolution fusion | flops 18866700288 | bytes 74858496 | tf_op jit(solution)/shard_map/transpose(jvp())/dot_general | solution.py:22
  567.8 33.9 %fusion.32 = bf16[896,2560]{1,0:T(8,128)(2,1)} fusion(bf16[4096,2560]{1,0:T(8,128)(2,1)} %convolution_convert_fusion.1, bf16[4096,896]{0,1:T(8,128)(2,1)} %get-tuple-element.27, f32[4096]{0:T(1024)S(1)} %copy-done.6, f32[4096,2560]{1,0:T(8,128)} %get-tuple-element.29), kind=kOutput, calls=%fused_computation.64 | convolution fusion | flops 18866700288 | bytes 74858496 | tf_op jit(solution)/shard_map/transpose(jvp())/dot_general | solution.py:22
  601.9 41.9 %fusion.33 = bf16[896,2560]{1,0:T(8,128)(2,1)} fusion(f32[4096,2560]{1,0:T(8,128)} %fusion.47, f32[4096,2560]{1,0:T(8,128)} %get-tuple-element.25, bf16[4096,2560]{1,0:T(8,128)(2,1)} %convolution_convert_fusion, bf16[1,4096,896]{1,2,0:T(8,128)(2,1)} %copy.20, f32[4096]{0:T(1024)S(1)} %copy-done.10), kind=kOutput, calls=%fused_computation.65 | convolution fusion | flops 18919129088 | bytes 116801536 | tf_op jit(solution)/shard_map/transpose(jvp())/dot_general | solution.py:21
  644.1 25.1 %convolution_convert_fusion.3 = bf16[896,2560]{1,0:T(8,128)(2,1)} fusion(bf16[4096,2560]{1,0:T(8,128)(2,1)} %get-tuple-element.28, bf16[4096,896]{0,1:T(8,128)(2,1)} %get-tuple-element.27, f32[4096]{0:T(1024)S(1)} %copy-done.6), kind=kOutput, calls=%fused_computation.68 | convolution fusion | flops 18801491968 | bytes 32915456 | tf_op jit(solution)/shard_map/transpose(jvp())/dot_general | solution.py:21
  669.3 3.5 fusion.57
  672.8 3.4 fusion.56
  676.2 35.0 %reduce-scatter.7.cloned.1.call-done = bf16[224,2560]{1,0:T(8,128)(2,1)} async-done(((bf16[896,2560]{1,0:T(8,128)(2,1)}), bf16[224,2560]{1,0:T(8,128)(2,1)}) %reduce-scatter.7.cloned.1.call-update) | async-done | bytes 1146896 | tf_op jit(solution)/shard_map/reduce_scatter | solution.py:53
  711.2 48.4 %reduce-scatter.9.cloned.1.call-done = bf16[224,2560]{1,0:T(8,128)(2,1)} async-done(((bf16[896,2560]{1,0:T(8,128)(2,1)}), bf16[224,2560]{1,0:T(8,128)(2,1)}) %reduce-scatter.9.cloned.1.call-update) | async-done | bytes 1146896 | tf_op jit(solution)/shard_map/reduce_scatter | solution.py:53
  759.6 3.4 fusion.55
  765.0 9.1 %psum.7 = f32[]{:T(128)} all-reduce(f32[]{:T(128)S(6)} %add.99), channel_id=1, replica_groups=mesh['rep'=4,'dp'=4] {'dp'}, use_global_device_ids=true, to_apply=%region_12.13 | all-reduce | flops 1 | bytes 8 | tf_op jit(solution)/shard_map/psum | solution.py:55
  774.8 8.7 %fusion.63 = (bf16[2,640,896]{2,1,0:T(8,128)(2,1)}, f32[2,640,896]{2,1,0:T(8,128)}, f32[2,640,896]{2,1,0:T(8,128)}) fusion(bf16[2,640,896]{2,1,0:T(8,128)(2,1)} %param.15, f32[]{:T(128)S(6)} %min_shard_map.3, bf16[1,640,896]{2,1,0:T(8,128)(2,1)} %bitcast.71, bf16[1,640,896]{2,1,0:T(8,128)(2,1)S(1)} %bitcast.69, f32[2,640,896]{2,1,0:T(8,128)} %param.21, ...), kind=kLoop, calls=%fused_computation.87 | loop fusion | flops 22937600 | bytes 25231364 | tf_op jit(solution)/shard_map/convert_element_type | solution.py:30
  783.6 14.7 %fusion.54 = (bf16[2,224,2560]{2,1,0:T(8,128)(2,1)}, f32[2,224,2560]{2,1,0:T(8,128)}, f32[2,224,2560]{2,1,0:T(8,128)}, bf16[2,224,2560]{2,1,0:T(8,128)(2,1)}, f3...) fusion(bf16[2,224,2560]{2,1,0:T(8,128)(2,1)S(1)} %copy-done, f32[]{:T(128)S(6)} %min_shard_map.3, ...), kind=kLoop, calls=%fused_computation.78 | loop fusion | flops 45875200 | bytes 50462724 | tf_op jit(solution)/shard_map/convert_element_type | solution.py:30
  (59 shorter events, 15.5 us)
Async XLA Ops:
  7.2 6.8 copy-start.2
  7.2 53.7 %all-gather.13.cloned.1.call-start = ((), (), s32[]{:S(2)}) async-start(), calls=%async_computation.12 | async-start | bytes 5734400 | tf_op jit(solution)/shard_map/all_gather | solution.py:40
  10.6 100.2 %all-gather.15.cloned.1.call-start = ((), (), s32[]{:S(2)}) async-start(), calls=%async_computation.13 | async-start | bytes 5734400 | tf_op jit(solution)/shard_map/all_gather | solution.py:40
  13.9 146.8 %all-gather.17.cloned.1.call-start = ((), (), s32[]{:S(2)}) async-start(), calls=%async_computation.14 | async-start | bytes 5734400 | tf_op jit(solution)/shard_map/all_gather | solution.py:40
  15.6 194.8 %all-gather.23.cloned.1.call-start = ((), (), s32[]{:S(2)}) async-start(), calls=%async_computation.17 | async-start | bytes 5734400 | tf_op jit(solution)/shard_map/all_gather | solution.py:40
  16.2 243.9 %all-gather.21.cloned.1.call-start = ((), (), s32[]{:S(2)}) async-start(), calls=%async_computation.16 | async-start | bytes 5734400 | tf_op jit(solution)/shard_map/all_gather | solution.py:40
  16.9 292.9 %all-gather.19.cloned.1.call-start = ((), (), s32[]{:S(2)}) async-start(), calls=%async_computation.15 | async-start | bytes 5734400 | tf_op jit(solution)/shard_map/all_gather | solution.py:40
  17.5 651.8 %reduce-scatter.15.cloned.1.call-start = ((), (), s32[]{:S(2)}) async-start(), calls=%async_computation.10 | async-start | bytes 5734400 | tf_op jit(solution)/shard_map/reduce_scatter | solution.py:53
  32.9 77.9 %copy-start.9 = (f32[4096]{0:T(1024)}, f32[4096]{0:T(1024)S(1)}, u32[]{:S(2)}) copy-start(f32[4096]{0:T(1024)S(1)} %add_rsqrt_fusion) | copy-start | bytes 49156
  187.5 0.6 copy-start.7
  188.1 241.9 %copy-start.5 = (f32[4096]{0:T(1024)}, f32[4096]{0:T(1024)S(1)}, u32[]{:S(2)}) copy-start(f32[4096]{0:T(1024)S(1)} %fusion.77) | copy-start | bytes 49156
  309.8 58.3 %copy-start.11 = (bf16[1,896,2560]{2,1,0:T(8,128)(2,1)S(1)}, bf16[1,896,2560]{2,1,0:T(8,128)(2,1)}, u32[]{:S(2)}) copy-start(bf16[1,896,2560]{2,1,0:T(8,128)(2,1)} %all-gather.19.cloned.1.call-done) | copy-start | bytes 13762564
  391.7 38.3 %copy-start.8 = (f32[4096]{0:T(1024)S(1)}, f32[4096]{0:T(1024)}, u32[]{:S(2)}) copy-start(f32[4096]{0:T(1024)} %copy-done.7) | copy-start | bytes 49156
  439.8 3.0 copy-start.3
  469.3 200.0 %reduce-scatter.17.cloned.1.call-start = ((), (), s32[]{:S(2)}) async-start(), calls=%async_computation.11 | async-start | bytes 5734400 | tf_op jit(solution)/shard_map/reduce_scatter | solution.py:53
  505.8 27.8 %copy-start.10 = (f32[4096]{0:T(1024)S(1)}, f32[4096]{0:T(1024)}, u32[]{:S(2)}) copy-start(f32[4096]{0:T(1024)} %copy-done.9) | copy-start | bytes 49156
  505.8 167.0 %reduce-scatter.11.cloned.1.call-start = ((), (), s32[]{:S(2)}) async-start(), calls=%async_computation.8 | async-start | bytes 5734400 | tf_op jit(solution)/shard_map/reduce_scatter | solution.py:53
  533.6 34.2 %copy-start.6 = (f32[4096]{0:T(1024)S(1)}, f32[4096]{0:T(1024)}, u32[]{:S(2)}) copy-start(f32[4096]{0:T(1024)} %copy-done.5) | copy-start | bytes 49156
  567.6 105.2 %reduce-scatter.13.cloned.1.call-start = ((), (), s32[]{:S(2)}) async-start(), calls=%async_computation.9 | async-start | bytes 5734400 | tf_op jit(solution)/shard_map/reduce_scatter | solution.py:53
  601.8 109.4 %reduce-scatter.7.cloned.1.call-start = ((), (), s32[]{:S(2)}) async-start(), calls=%async_computation.6 | async-start | bytes 5734400 | tf_op jit(solution)/shard_map/reduce_scatter | solution.py:53
  643.8 115.8 %reduce-scatter.9.cloned.1.call-start = ((), (), s32[]{:S(2)}) async-start(), calls=%async_computation.7 | async-start | bytes 5734400 | tf_op jit(solution)/shard_map/reduce_scatter | solution.py:53
  669.3 105.5 %copy-start.4 = (bf16[640,896]{1,0:T(8,128)(2,1)S(1)}, bf16[640,896]{1,0:T(8,128)(2,1)}, u32[]{:S(2)}) copy-start(bf16[640,896]{1,0:T(8,128)(2,1)} %reduce-scatter.15.cloned.1.call-done) | copy-start | bytes 3440644
  774.8 8.8 %copy-start = (bf16[2,224,2560]{2,1,0:T(8,128)(2,1)S(1)}, bf16[2,224,2560]{2,1,0:T(8,128)(2,1)}, u32[]{:S(2)}) copy-start(bf16[2,224,2560]{2,1,0:T(8,128)(2,1)} %param.13) | copy-start | bytes 6881284
  774.8 8.8 %copy-start.1 = (bf16[2,224,2560]{2,1,0:T(8,128)(2,1)S(1)}, bf16[2,224,2560]{2,1,0:T(8,128)(2,1)}, u32[]{:S(2)}) copy-start(bf16[2,224,2560]{2,1,0:T(8,128)(2,1)} %param.14) | copy-start | bytes 6881284
Sparse Core Ops, SparseCore 0:
  10.7 50.1 all-gather.12
  63.0 47.6 all-gather.14
  112.9 47.6 all-gather.16
  162.6 47.6 all-gather.22
  212.3 47.6 all-gather.20
  262.1 47.6 all-gather.18
  469.4 46.4 reduce-scatter.14
  518.8 45.6 reduce-scatter.16
  567.7 46.4 reduce-scatter.10
  616.9 45.6 reduce-scatter.12
  665.5 45.6 reduce-scatter.6
  713.9 45.6 reduce-scatter.8
where the time goes:
time: 813 us; the launch traced here: 805 us
  matrix products  509 us (63%)
  waiting for transfers between devices  187 us (23%)
  other arithmetic  48.1 us (6%)
  local copies, waits for them, and re-layouts  33.1 us (4%)
  between operations  17.3 us (2%)
  blocking collectives  9.14 us (1%)
    dot_general x5, matrix products, layer(): up = jnp.dot(a, w['w_up'], preferred_element_type=jnp.float32)  186 us
    dot_general x5, matrix products, layer(): gate = jnp.dot(a, w['w_gate'], preferred_element_type=jnp.float32)  178 us
    dot_general x5, matrix products, matmul(): jnp.dot(a, w, preferred_element_type=jnp.float32).astype(jnp.bfloat16)  145 us
    all_gather x6, waiting for transfers between devices, fetched(): lax.all_gather(w[number], 'dp', axis=0, tiled=True)  101 us
    reduce_scatter x6, waiting for transfers between devices, step(): lax.psum_scatter(by_w[name], 'dp', scatter_dimension=0, tiled=True)  83.5 us
    unnamed x26, local copies, waits for them, and re-layouts  25.1 us
    convert_element_type x2, other arithmetic, adamw(): return ((w - 0.02 * step).astype(jnp.bfloat16), m, v)  23.5 us
  transfers between devices with their start and end apart: 12, of which 7 were waited for; matrix products, arithmetic and copies ran while one was open for 50% of the time, Pallas kernels for 0%

commit v1 on v0

v1 whole, which is shorter than its diff:
```python
import functools

import jax
import jax.numpy as jnp
from jax import lax
from jax.experimental import pallas as pl
from jax.experimental.pallas import tpu as pltpu
from jax.sharding import PartitionSpec as P

MESH = pl.DeviceIdType.MESH
ANY = pl.BlockSpec(memory_space=pl.ANY)
F32, BF16 = jnp.float32, jnp.bfloat16
VMEM_LIMIT = 60 * 1024 * 1024
ROWS = 512
COLS = 256


def dot(a, b, dims=((1,), (0,))):
    return lax.dot_general(a, b, (dims, ((), ())), preferred_element_type=F32)


NT = ((1,), (1,))


def inv_rms(wide):
    return lax.rsqrt(jnp.mean(wide * wide, -1, keepdims=True) + 1e-6)


def normed(h):
    wide = h.astype(F32)
    return (wide * inv_rms(wide)).astype(BF16)


class Gather:
    def __init__(self, n, shards, fulls, stages, local_sem, send_sem, recv_sem):
        self.me, rep = lax.axis_index("dp"), lax.axis_index("rep")
        self.n, self.p = n, lax.rem(rep, 2)
        self.right, self.left = {"dp": lax.rem(self.me + 1, n)}, {"dp": lax.rem(self.me + n - 1, n)}
        self.partner = {"rep": rep + 1 - 2 * self.p}
        self.shards, self.fulls, self.stages = shards, fulls, stages
        self.local_sem, self.send_sem, self.recv_sem = local_sem, send_sem, recv_sem

    def barrier(self):
        sem = pltpu.get_barrier_semaphore()
        for device in (self.left, self.right, self.partner):
            pl.semaphore_signal(sem, inc=1, device_id=device, device_id_type=MESH)
        pl.semaphore_wait(sem, 3)

    def half(self, k, away, part=None):
        rows, columns = self.shards[k].shape
        owner = lax.rem(self.me + away + self.n, self.n)
        start = pl.multiple_of(owner * rows + self.p * (rows // 2), 16)
        if part is None:
            return self.fulls[k].at[pl.ds(start, rows // 2)]
        if columns % 256 == 0:
            return self.fulls[k].at[pl.ds(start, rows // 2), pl.ds(part * (columns // 2), columns // 2)]
        quarter = rows // 4
        return self.fulls[k].at[pl.ds(pl.multiple_of(start + part * quarter, 16), quarter)]

    def copy(self, k, slot, src, dst, device):
        return pltpu.make_async_remote_copy(src_ref=src, dst_ref=dst, send_sem=self.send_sem.at[k, slot], recv_sem=self.recv_sem.at[k, slot], device_id=device, device_id_type=MESH)

    def first(self, k, side):
        rows = self.shards[k].shape[0]
        own = self.shards[k].at[pl.ds(pl.multiple_of(self.p * (rows // 2), 16), rows // 2)]
        return self.copy(k, side, own, self.half(k, 0), self.left if side else self.right)

    def second(self, k, side):
        place = self.half(k, 1 if side else -1, side)
        return self.copy(k, 2 + side, place, place, self.left if side else self.right)

    def over(self, k, which):
        place = self.half(k, (-1, 1, 2)[which])
        return self.copy(k, 4 + which, place, place, self.partner)

    def load(self, k):
        return pltpu.make_async_copy(self.shards[k], self.stages[k], self.local_sem.at[k, 0])

    def store(self, k):
        rows = self.shards[k].shape[0]
        place = self.fulls[k].at[pl.ds(pl.multiple_of(self.me * rows, 16), rows)]
        return pltpu.make_async_copy(self.stages[k], place, self.local_sem.at[k, 1])

    def start(self, k):
        self.first(k, 0).start()
        self.first(k, 1).start()
        self.load(k).start()

    def keep(self, k):
        self.load(k).wait()
        self.store(k).start()

    def forward(self, k):
        for side in (0, 1):
            self.first(k, side).wait_recv()
            self.second(k, side).start()
        self.over(k, 0).start()
        self.over(k, 1).start()

    def last(self, k):
        self.second(k, 0).wait_recv()
        self.second(k, 1).wait_recv()
        self.over(k, 2).start()

    def finish(self, k):
        self.store(k).wait()
        for which in range(3):
            self.over(k, which).wait()
        for side in (0, 1):
            self.first(k, side).wait_send()
            self.second(k, side).wait_send()


def gather_scratch(weights):
    k = len(weights)
    return [pltpu.VMEM(w.shape[1:], w.dtype) for w in weights] + [pltpu.SemaphoreType.DMA((k, 2)), pltpu.SemaphoreType.DMA((k, 7)), pltpu.SemaphoreType.DMA((k, 7))]


def fulls_of(n, weights):
    return [jax.ShapeDtypeStruct((n * w.shape[1], w.shape[2]), w.dtype) for w in weights]


def gather_kernel(n, *refs):
    k = (len(refs) - 3) // 3
    g = Gather(n, [s.at[0] for s in refs[:k]], refs[k : 2 * k], refs[2 * k : 3 * k], *refs[3 * k :])
    g.barrier()
    for phase in (g.start, g.keep, g.forward, g.last, g.finish):
        for one in range(k):
            phase(one)


def gathered(n, weights):
    k = len(weights)
    sent = sum(3 * w.shape[1] * w.shape[2] for w in weights)
    return pl.pallas_call(
        functools.partial(gather_kernel, n),
        out_shape=fulls_of(n, weights),
        in_specs=[ANY] * k,
        out_specs=[ANY] * k,
        scratch_shapes=gather_scratch(weights),
        compiler_params=pltpu.CompilerParams(collective_id=0, has_side_effects=True, vmem_limit_bytes=16 * 1024 * 1024),
        cost_estimate=pl.CostEstimate(flops=40_000_000_000, bytes_accessed=8 * sent, transcendentals=0),
        name="gather",
    )(*weights)


def whole(array):
    return pl.BlockSpec(array.shape, lambda i: (0,) * len(array.shape), pipeline_mode=pl.Buffered(1))


def rows_of(d):
    return pl.BlockSpec((ROWS, d), lambda i: (i, 0))


def columns_of(d):
    return pl.BlockSpec((d, ROWS), lambda i: (0, i))


def part_of(array, dim, half):
    shape = tuple(s // 2 if i == dim else s for i, s in enumerate(array.shape))
    place = tuple(half if i == dim else 0 for i in range(2))
    return pl.BlockSpec(shape, lambda i: place, pipeline_mode=pl.Buffered(1))


def params(**more):
    return pltpu.CompilerParams(dimension_semantics=("arbitrary",), vmem_limit_bytes=VMEM_LIMIT, **more)


def beside(g, k, steps, forwards):
    i = pl.program_id(0)

    @pl.when(i == 0)
    def _():
        g.barrier()
        for one in range(k):
            g.start(one)

    @pl.when(i == 1)
    def _():
        for one in range(k):
            g.keep(one)

    for one, at in enumerate(forwards):

        @pl.when(i == at)
        def _(one=one):
            g.forward(one)


def after(g, k, steps):
    @pl.when(pl.program_id(0) == steps - 1)
    def _():
        for phase in (g.last, g.finish):
            for one in range(k):
                phase(one)


def up_kernel(n, layers, steps, x_ref, wg_ref, wu_ref, *refs):
    k = len(layers)
    shards, (gate_ref, up_ref, act_ref, at_ref), refs = refs[:k], refs[k : k + 4], refs[k + 4 :]
    g = Gather(n, [s.at[layer] for s, layer in zip(shards, layers)], refs[:k], refs[k : 2 * k], *refs[2 * k :])
    beside(g, k, steps, (2, 5))
    a = normed(x_ref[...])
    at_ref[...] = a.T
    for c in range(wg_ref.shape[1] // COLS):
        cols = pl.ds(c * COLS, COLS)
        gate = dot(a, wg_ref[:, cols])
        up = dot(a, wu_ref[:, cols])
        gate_ref[:, cols] = gate
        up_ref[:, cols] = up
        act_ref[:, cols] = (gate * jax.nn.sigmoid(gate) * up).astype(BF16)
    after(g, k, steps)


def up_part(n, x, full, weights, layers):
    tokens, d = x.shape
    ff, k = full[0].shape[1], len(weights)
    steps = tokens // ROWS
    wide = jax.ShapeDtypeStruct((tokens, ff), F32)
    return pl.pallas_call(
        functools.partial(up_kernel, n, layers, steps),
        grid=(steps,),
        out_shape=[wide, wide, jax.ShapeDtypeStruct((tokens, ff), BF16), jax.ShapeDtypeStruct((d, tokens), BF16), *fulls_of(n, weights)],
        in_specs=[rows_of(d), whole(full[0]), whole(full[1])] + [ANY] * k,
        out_specs=[rows_of(ff)] * 3 + [columns_of(d)] + [ANY] * k,
        scratch_shapes=gather_scratch(weights),
        compiler_params=params(collective_id=1, has_side_effects=True),
        cost_estimate=pl.CostEstimate(flops=4 * tokens * d * ff, bytes_accessed=10 * tokens * ff, transcendentals=tokens * ff),
        name="up",
    )(x, *full, *weights)


def down_kernel(n, layers, steps, x_ref, act_ref, wd_ref, *refs):
    k = len(layers)
    shards, (h_ref, at_ref), refs = refs[:k], refs[k : k + 2], refs[k + 2 :]
    g = Gather(n, [s.at[layer] for s, layer in zip(shards, layers)], refs[:k], refs[k : 2 * k], *refs[2 * k :])
    beside(g, k, steps, (4, 7))
    h = x_ref[...] + dot(act_ref[...], wd_ref[...]).astype(BF16)
    h_ref[...] = h
    at_ref[...] = normed(h).T
    after(g, k, steps)


def down_part(n, x, act, full, weights, layers):
    tokens, d = x.shape
    ff, k = act.shape[1], len(weights)
    steps = tokens // ROWS
    return pl.pallas_call(
        functools.partial(down_kernel, n, layers, steps),
        grid=(steps,),
        out_shape=[jax.ShapeDtypeStruct((tokens, d), BF16), jax.ShapeDtypeStruct((d, tokens), BF16), *fulls_of(n, weights)],
        in_specs=[rows_of(d), rows_of(ff), whole(full)] + [ANY] * k,
        out_specs=[rows_of(d), columns_of(d)] + [ANY] * k,
        scratch_shapes=gather_scratch(weights),
        compiler_params=params(collective_id=2, has_side_effects=True),
        cost_estimate=pl.CostEstimate(flops=2 * tokens * d * ff, bytes_accessed=2 * tokens * ff + 6 * tokens * d, transcendentals=0),
        name="down",
    )(x, act, full, *weights)


def by_hidden(gate, up, dact, s):
    silu = gate * s
    return (dact * up * (s + silu * (1 - s))).astype(BF16), (dact * silu).astype(BF16)


def hidden_kernel(h_ref, dy_ref, wg_ref, wu_ref, wd_ref, act_ref, dg_ref, du_ref, *dyt_ref):
    a, dy = normed(h_ref[...]), dy_ref[...]
    for ref in dyt_ref:
        ref[...] = dy.T
    for c in range(wg_ref.shape[1] // COLS):
        cols = pl.ds(c * COLS, COLS)
        gate = dot(a, wg_ref[:, cols])
        up = dot(a, wu_ref[:, cols])
        dact = dot(dy, wd_ref[cols, :], NT).astype(BF16).astype(F32)
        s = jax.nn.sigmoid(gate)
        act_ref[:, cols] = (gate * s * up).astype(BF16)
        dg_ref[:, cols], du_ref[:, cols] = by_hidden(gate, up, dact, s)


def hidden(h, dy, full, half):
    tokens, d = h.shape
    ff = full[0].shape[1] // 2
    wide = jax.ShapeDtypeStruct((tokens, ff), BF16)
    return pl.pallas_call(
        hidden_kernel,
        grid=(tokens // ROWS,),
        out_shape=[wide] * 3 + [jax.ShapeDtypeStruct((d, tokens), BF16)] * half,
        in_specs=[rows_of(d), rows_of(d), part_of(full[0], 1, half), part_of(full[1], 1, half), part_of(full[2], 0, half)],
        out_specs=[rows_of(ff)] * 3 + [columns_of(d)] * half,
        compiler_params=params(),
        cost_estimate=pl.CostEstimate(flops=6 * tokens * d * ff, bytes_accessed=4 * tokens * d + 6 * tokens * ff + 6 * d * ff, transcendentals=tokens * ff),
        name="hidden",
    )(h, dy, *full)


def kept_kernel(gate_ref, up_ref, dy_ref, wd_ref, dg_ref, du_ref):
    dy = dy_ref[...]
    for c in range(gate_ref.shape[1] // COLS):
        cols = pl.ds(c * COLS, COLS)
        gate = gate_ref[:, cols]
        dact = dot(dy, wd_ref[cols, :], NT).astype(BF16).astype(F32)
        dg_ref[:, cols], du_ref[:, cols] = by_hidden(gate, up_ref[:, cols], dact, jax.nn.sigmoid(gate))


def kept_hidden(gate, up, dy, full, half):
    tokens, d = dy.shape
    ff = gate.shape[1] // 2
    wide = jax.ShapeDtypeStruct((tokens, ff), BF16)
    block = pl.BlockSpec((ROWS, ff), lambda i: (i, half))
    return pl.pallas_call(
        kept_kernel,
        grid=(tokens // ROWS,),
        out_shape=[wide] * 2,
        in_specs=[block, block, rows_of(d), part_of(full, 0, half)],
        out_specs=[rows_of(ff)] * 2,
        compiler_params=params(),
        cost_estimate=pl.CostEstimate(flops=2 * tokens * d * ff, bytes_accessed=2 * tokens * d + 12 * tokens * ff + 2 * d * ff, transcendentals=tokens * ff),
        name="kept_hidden",
    )(gate, up, dy, full)


def gradient_kernel(turn, counts, at_ref, *refs):
    k = len(counts)
    i, first = pl.program_id(0), 0
    for one, count in enumerate(counts):

        @pl.when(jnp.logical_and(i >= first, i < first + count))
        def _(d_ref=refs[one]):
            out = dot(at_ref[...], d_ref[...])
            refs[k][...] = (out.T if turn else out).astype(BF16)

        first += count


def gradient(at, ds, turn=False):
    rows, tokens = at.shape
    cols = 256
    counts = [d.shape[1] // cols for d in ds]
    firsts = [sum(counts[:one]) for one in range(len(ds))]
    ff = sum(d.shape[1] for d in ds)

    def along(height, one):
        return pl.BlockSpec((height, cols), lambda i: (0, jnp.clip(i - firsts[one], 0, counts[one] - 1)))

    shape, out = (ff, rows), pl.BlockSpec((cols, rows), lambda i: (i, 0))
    if not turn:
        shape, out = (rows, ff), pl.BlockSpec((rows, cols), lambda i: (0, i))
    return pl.pallas_call(
        functools.partial(gradient_kernel, turn, counts),
        grid=(sum(counts),),
        out_shape=jax.ShapeDtypeStruct(shape, BF16),
        in_specs=[whole(at)] + [along(tokens, one) for one in range(len(ds))],
        out_specs=out,
        compiler_params=params(),
        cost_estimate=pl.CostEstimate(flops=2 * tokens * rows * ff, bytes_accessed=2 * (rows * tokens + ff * tokens + rows * ff), transcendentals=0),
        name="gradient",
    )(at, *ds)


def states_kernel(dga_ref, dgb_ref, dua_ref, dub_ref, h_ref, dy_ref, wg_ref, wu_ref, dh_ref, dht_ref):
    ff = dga_ref.shape[1]

    def through(a_ref, b_ref, w_ref):
        return (dot(a_ref[...], w_ref[:, :ff], NT) + dot(b_ref[...], w_ref[:, ff:], NT)).astype(BF16)

    da = (through(dga_ref, dgb_ref, wg_ref) + through(dua_ref, dub_ref, wu_ref)).astype(F32)
    wide = h_ref[...].astype(F32)
    scale = inv_rms(wide)
    by_scale = jnp.sum(da * wide, -1, keepdims=True)
    dh = da * scale - (by_scale * scale * scale * scale / wide.shape[-1]) * wide
    dh = dy_ref[...] + dh.astype(BF16)
    dh_ref[...] = dh
    dht_ref[...] = dh.T


def states(dg, du, h, dy, full):
    tokens, d = h.shape
    ff = dg[0].shape[1]
    return pl.pallas_call(
        states_kernel,
        grid=(tokens // ROWS,),
        out_shape=[jax.ShapeDtypeStruct((tokens, d), BF16), jax.ShapeDtypeStruct((d, tokens), BF16)],
        in_specs=[rows_of(ff)] * 4 + [rows_of(d), rows_of(d), whole(full[0]), whole(full[1])],
        out_specs=[rows_of(d), columns_of(d)],
        compiler_params=params(),
        cost_estimate=pl.CostEstimate(flops=8 * tokens * d * ff, bytes_accessed=8 * tokens * ff + 8 * tokens * d + 8 * d * ff, transcendentals=tokens),
        name="states",
    )(*dg, *du, h, dy, full[0], full[1])


def adamw(w, m, v, g):
    m = 0.9 * m + 0.1 * g
    v = 0.95 * v + 0.05 * g * g
    step = m * lax.rsqrt(v + 1e-8) + 0.1 * w
    return (w - 0.02 * step).astype(BF16), m, v


def clipped(gradients, sum_of_squares, count):
    factor = jnp.minimum(1.0, 0.5 * lax.rsqrt(sum_of_squares / count + 1e-30))
    return [g * factor for g in gradients]


def solution(mesh):
    n = mesh.shape["dp"]

    def scattered(g):
        return lax.psum_scatter(g, "dp", scatter_dimension=0, tiled=True)

    def follow(array, *earlier):
        return lax.optimization_barrier((array, *earlier))[0]

    def step(x, dy, *arrays):
        weights, m, v = (arrays[i : i + 3] for i in (0, 3, 6))
        x, dy = x[0], dy[0]
        w_gate, w_up, w_down = weights
        full = gathered(n, (w_gate, w_up))
        gate, up, act, at0, down0, gate1 = up_part(n, x, full, (w_down, w_gate), (0, 1))
        h, at1, up1, down1 = down_part(n, x, act, down0, (w_up, w_down), (1, 1))
        full1 = gate1, up1, down1

        act_a, dg_a, du_a = hidden(h, dy, full1, 0)
        one_a = gradient(at1, (dg_a, du_a))
        sum_a = scattered(one_a)
        act_b, dg_b, du_b, dyt = hidden(follow(h, one_a), dy, full1, 1)
        one_b = gradient(at1, (dg_b, du_b))
        sum_b = scattered(one_b)
        one_down = gradient(follow(dyt, one_b), (act_a, act_b), True)
        sum_down = scattered(one_down)
        dh, dht = states((dg_a, dg_b), (du_a, du_b), follow(h, one_down, sum_a), dy, full1)
        down = gradient(dht, (act,), True)
        last_down = scattered(down)
        dg_a, du_a = kept_hidden(gate, up, follow(dh, down, sum_b), down0, 0)
        a = gradient(at0, (dg_a, du_a))
        last_a = scattered(a)
        dg_b, du_b = kept_hidden(gate, up, follow(dh, a, sum_down), down0, 1)
        last_b = scattered(gradient(follow(at0, last_down), (dg_b, du_b)))

        sums = sum_a, sum_b, sum_down, last_down, last_a, last_b
        squares = lax.psum(sum(jnp.sum(lax.optimization_barrier(g).astype(F32) ** 2) for g in sums), "dp")

        def joined(a, b, side):
            half = a.shape[1] // 2
            return jnp.concatenate([one[:, side * half : (side + 1) * half] for one in (a, b)], -1)

        pairs = (last_a, last_b), (sum_a, sum_b)
        gradients = [jnp.stack([joined(a, b, side) for a, b in pairs]).astype(F32) for side in range(2)]
        gradients.append(jnp.stack([last_down, sum_down]).astype(F32))
        gradients = clipped(gradients, squares, lax.psum(1, "dp") * sum(g.size for g in gradients))
        new = [adamw(w.astype(F32), m, v, g) for w, m, v, g in zip(weights, m, v, gradients, strict=True)]
        return tuple(one[which] for which in range(3) for one in new)

    spec, cut = P(("rep", "dp"), None, None), P(None, "dp", None)
    return jax.shard_map(
        step,
        mesh=mesh,
        in_specs=(spec, spec) + (cut,) * 9,
        out_specs=(P("rep", "dp", None),) * 9,
        check_vma=False,
    )
```

time: 813 us -> 634 us (0.78)
  Pallas kernels: 0 us -> 514 us
  matrix products: 509 us -> 0 us
  waiting for transfers between devices: 187 us -> 29.9 us
  local copies, waits for them, and re-layouts: 33.1 us -> 14.3 us
  other arithmetic: 48.1 us -> 38.3 us
    pallas_call x0 -> x14, Pallas kernels: none -> 514 us  [the longest x6 158 us: gradient(): pl.pallas_call(functools.partial(gradient_kernel, turn, counts), grid=(su...]
    dot_general x15 -> x0, matrix products: 509 us -> none  [the longest x5 186 us: layer(): up = jnp.dot(a, w['w_up'], preferred_element_type=jnp.float32)]
    all_gather x6 -> x0, waiting for transfers between devices: 101 us -> none  [fetched(): lax.all_gather(w[number], 'dp', axis=0, tiled=True)]
    reduce_scatter x6, waiting for transfers between devices: 83.5 us -> 29.5 us  [scattered(): return lax.psum_scatter(g, 'dp', scatter_dimension=0, tiled=True)]
    unnamed x26 -> x20, local copies, waits for them, and re-layouts: 25.1 us -> 8.78 us
    add_any x1 -> x0, other arithmetic: 9.79 us -> none  [normed(): wide = h.astype(jnp.float32)]
  transfers between devices with their start and end apart: 12 -> 6, of which waited for: 7 -> 1; matrix products, arithmetic and copies ran while one was open for 50% -> 2% of each run, Pallas kernels for 0% -> 46%
where the time goes in v1:
time: 634 us; the launch traced here: 626 us
  Pallas kernels  514 us (81%)
  other arithmetic  38.3 us (6%)
  waiting for transfers between devices  29.9 us (5%)
  between operations  19.4 us (3%)
  local copies, waits for them, and re-layouts  14.3 us (2%)
  blocking collectives  9.41 us (1%)
    pallas_call x6, Pallas kernels, gradient(): pl.pallas_call(functools.partial(gradient_kernel, turn, counts), grid=(su...  158 us
    pallas_call x2, Pallas kernels, hidden(): pl.pallas_call(hidden_kernel, grid=(tokens // ROWS,), out_shape=[wide] *...  83.4 us
    pallas_call x1, Pallas kernels, up_part(): pl.pallas_call(functools.partial(up_kernel, n, layers, steps), grid=(step...  63.9 us
    pallas_call x2, Pallas kernels, kept_hidden(): pl.pallas_call(kept_kernel, grid=(tokens // ROWS,), out_shape=[wide] * 2,...  59.6 us
    pallas_call x1, Pallas kernels, states(): pl.pallas_call(states_kernel, grid=(tokens // ROWS,), out_shape=[jax.Shap...  57.5 us
    pallas_call x1, Pallas kernels, down_part(): pl.pallas_call(functools.partial(down_kernel, n, layers, steps), grid=(st...  47.6 us
    pallas_call x1, Pallas kernels, gathered(): pl.pallas_call(functools.partial(gather_kernel, n), out_shape=fulls_of(n,...  44 us
    reduce_scatter x6, waiting for transfers between devices, scattered(): return lax.psum_scatter(g, 'dp', scatter_dimension=0, tiled=True)  29.5 us
  transfers between devices with their start and end apart: 6, of which 1 were waited for; matrix products, arithmetic and copies ran while one was open for 2% of the time, Pallas kernels for 46%

profile of v1, /device:TPU:112, one launch (start us, length us, event | category | flops | bytes accessed | tf_op | source)
XLA Modules:
  0.0 625.7 jit_solution(10070886896031759020)
XLA Ops:
  7.3 1.6 copy-done
  8.9 1.6 copy-done.2
  10.6 44.0 %gather.1 = (bf16[896,2560]{1,0:T(8,128)(2,1)S(1)}, bf16[896,2560]{1,0:T(8,128)(2,1)S(1)}) custom-call(bf16[2,224,2560]{2,1,0:T(8,128)(2,1)S(1)} %copy-done, bf16[2,224,2560]{2,1,0:T(8,128)(2,1)S(1)} %copy-done.2), custom_call_target="tpu_custom_call" | custom-call | flops 40000000000 | bytes 27525120 | tf_op jit(solution)/shard_map/gather/pallas_call | solution.py:135
  54.6 2.1 copy-done.4
  56.7 2.1 copy-done.5
  58.9 63.9 %up.1 = (f32[4096,2560]{1,0:T(8,128)}, f32[4096,2560]{1,0:T(8,128)}, bf16[4096,2560]{1,0:T(8,128)(2,1)}, bf16[896,4096]{1,0:T(8,128)(2,1)}, bf16[2560,896]{1,0:T(8,128)(2,1)}, /*index=5*/bf16[896,2560]{1,0:T(8,128)(2,1)}) custom-call(bf16[4096,896]{1,0:T(8,128)(2,1)} %bitcast.14, bf16[896,2560]{1,0:T(8,128)(2,1)} %copy-done.4, bf16[896,2560]{1,0:T(8,128)(2,1)} %copy-done.5, ...), custom_call_target="tpu_custom_call" | custom-call | flops 37580963840 | bytes 104857600 | tf_op jit(solution)/shard_map/up/pallas_call | solution.py:220
  122.8 47.6 %down.1 = (bf16[4096,896]{1,0:T(8,128)(2,1)}, bf16[896,4096]{1,0:T(8,128)(2,1)}, bf16[896,2560]{1,0:T(8,128)(2,1)}, bf16[2560,896]{1,0:T(8,128)(2,1)}) custom-call(bf16[4096,896]{1,0:T(8,128)(2,1)} %bitcast.15, bf16[4096,2560]{1,0:T(8,128)(2,1)} %get-tuple-element.45.act_ref.refs_0_, bf16[2560,896]{1,0:T(8,128)(2,1)} %get-tuple-element.46.wd_ref, ...), custom_call_target="tpu_custom_call" | custom-call | flops 18790481920 | bytes 42991616 | tf_op jit(solution)/shard_map/down/pallas_call | solution.py:248
  170.4 41.5 %hidden.2 = (bf16[4096,1280]{1,0:T(8,128)(2,1)}, bf16[4096,1280]{1,0:T(8,128)(2,1)}, bf16[4096,1280]{1,0:T(8,128)(2,1)}) custom-call(bf16[4096,896]{1,0:T(8,128)(2,1)} %get-tuple-element.61.h_ref, bf16[4096,896]{1,0:T(8,128)(2,1)} %bitcast.16, bf16[896,2560]{1,0:T(8,128)(2,1)} %get-tuple-element.48.wg_ref, bf16[896,2560]{1,0:T(8,128)(2,1)} %get-tuple-element.49.wu_ref, ...), custom_call_target="tpu_custom_call" | custom-call | flops 28185722880 | bytes 53018624 | tf_op jit(solution)/shard_map/hidden/pallas_call | solution.py:284
  211.9 26.3 %gradient.6 = bf16[896,2560]{1,0:T(8,128)(2,1)} custom-call(bf16[896,4096]{1,0:T(8,128)(2,1)} %get-tuple-element.52.at_ref, bf16[4096,1280]{1,0:T(8,128)(2,1)} %get-tuple-element.51.refs_0_.dga_ref, bf16[4096,1280]{1,0:T(8,128)(2,1)} %get-tuple-element.53.refs_1_.dua_ref), custom_call_target="tpu_custom_call" | custom-call | flops 18790481920 | bytes 32899072 | tf_op jit(solution)/shard_map/gradient/pallas_call | solution.py:348
  238.4 41.8 %hidden.3 = (bf16[4096,1280]{1,0:T(8,128)(2,1)}, bf16[4096,1280]{1,0:T(8,128)(2,1)}, bf16[4096,1280]{1,0:T(8,128)(2,1)}, bf16[896,4096]{1,0:T(8,128)(2,1)}) custom-call(bf16[4096,896]{1,0:T(8,128)(2,1)} %get-tuple-element.61.h_ref, bf16[4096,896]{1,0:T(8,128)(2,1)} %bitcast.17, bf16[896,2560]{1,0:T(8,128)(2,1)} %get-tuple-element.48.wg_ref, ...), custom_call_target="tpu_custom_call" | custom-call | flops 28185722880 | bytes 53018624 | tf_op jit(solution)/shard_map/hidden/pallas_call | solution.py:284
  280.2 26.2 %gradient.7 = bf16[896,2560]{1,0:T(8,128)(2,1)} custom-call(bf16[896,4096]{1,0:T(8,128)(2,1)} %get-tuple-element.52.at_ref, bf16[4096,1280]{1,0:T(8,128)(2,1)} %get-tuple-element.55.refs_0_.dgb_ref, bf16[4096,1280]{1,0:T(8,128)(2,1)} %get-tuple-element.56.refs_1_.dub_ref), custom_call_target="tpu_custom_call" | custom-call | flops 18790481920 | bytes 32899072 | tf_op jit(solution)/shard_map/gradient/pallas_call | solution.py:348
  306.5 27.1 %gradient.8 = bf16[2560,896]{1,0:T(8,128)(2,1)} custom-call(bf16[896,4096]{1,0:T(8,128)(2,1)} %get-tuple-element.58.at_ref, bf16[4096,1280]{1,0:T(8,128)(2,1)} %get-tuple-element.59.refs_0_, bf16[4096,1280]{1,0:T(8,128)(2,1)} %get-tuple-element.60.refs_1_), custom_call_target="tpu_custom_call" | custom-call | flops 18790481920 | bytes 32899072 | tf_op jit(solution)/shard_map/gradient/pallas_call | solution.py:348
  333.8 57.5 %states.1 = (bf16[4096,896]{1,0:T(8,128)(2,1)}, bf16[896,4096]{1,0:T(8,128)(2,1)}) custom-call(bf16[4096,1280]{1,0:T(8,128)(2,1)} %get-tuple-element.51.refs_0_.dga_ref, bf16[4096,1280]{1,0:T(8,128)(2,1)} %get-tuple-element.55.refs_0_.dgb_ref, bf16[4096,1280]{1,0:T(8,128)(2,1)} %get-tuple-element.53.refs_1_.dua_ref, ...), custom_call_target="tpu_custom_call" | custom-call | flops 37580963840 | bytes 80478208 | tf_op jit(solution)/shard_map/states/pallas_call | solution.py:379
  391.3 26.1 %gradient.9 = bf16[2560,896]{1,0:T(8,128)(2,1)} custom-call(bf16[896,4096]{1,0:T(8,128)(2,1)} %get-tuple-element.63.at_ref, bf16[4096,2560]{1,0:T(8,128)(2,1)} %get-tuple-element.45.act_ref.refs_0_), custom_call_target="tpu_custom_call" | custom-call | flops 18790481920 | bytes 32899072 | tf_op jit(solution)/shard_map/gradient/pallas_call | solution.py:348
  417.5 30.0 %kept_hidden.2 = (bf16[4096,1280]{1,0:T(8,128)(2,1)}, bf16[4096,1280]{1,0:T(8,128)(2,1)}) custom-call(f32[4096,2560]{1,0:T(8,128)} %get-tuple-element.43.gate_ref, f32[4096,2560]{1,0:T(8,128)} %get-tuple-element.44.up_ref, bf16[4096,896]{1,0:T(8,128)(2,1)} %get-tuple-element.68.dy_ref, bf16[2560,896]{1,0:T(8,128)(2,1)} %get-tuple-element.46.wd_ref), custom_call_target="tpu_custom_call" | custom-call | flops 9395240960 | bytes 72548352 | tf_op jit(solution)/shard_map/kept_hidden/pallas_call | solution.py:310
  447.5 26.2 %gradient.10 = bf16[896,2560]{1,0:T(8,128)(2,1)} custom-call(bf16[896,4096]{1,0:T(8,128)(2,1)} %get-tuple-element.67.at_ref, bf16[4096,1280]{1,0:T(8,128)(2,1)} %get-tuple-element.65.refs_0_, bf16[4096,1280]{1,0:T(8,128)(2,1)} %get-tuple-element.66.refs_1_), custom_call_target="tpu_custom_call" | custom-call | flops 18790481920 | bytes 32899072 | tf_op jit(solution)/shard_map/gradient/pallas_call | solution.py:348
  473.8 29.7 %kept_hidden.3 = (bf16[4096,1280]{1,0:T(8,128)(2,1)}, bf16[4096,1280]{1,0:T(8,128)(2,1)}) custom-call(f32[4096,2560]{1,0:T(8,128)} %get-tuple-element.43.gate_ref, f32[4096,2560]{1,0:T(8,128)} %get-tuple-element.44.up_ref, bf16[4096,896]{1,0:T(8,128)(2,1)} %get-tuple-element.68.dy_ref, bf16[2560,896]{1,0:T(8,128)(2,1)} %get-tuple-element.46.wd_ref), custom_call_target="tpu_custom_call" | custom-call | flops 9395240960 | bytes 72548352 | tf_op jit(solution)/shard_map/kept_hidden/pallas_call | solution.py:310
  503.5 26.2 %gradient.11 = bf16[896,2560]{1,0:T(8,128)(2,1)} custom-call(bf16[896,4096]{1,0:T(8,128)(2,1)} %get-tuple-element.67.at_ref, bf16[4096,1280]{1,0:T(8,128)(2,1)} %get-tuple-element.69.refs_0_, bf16[4096,1280]{1,0:T(8,128)(2,1)} %get-tuple-element.70.refs_1_), custom_call_target="tpu_custom_call" | custom-call | flops 18790481920 | bytes 32899072 | tf_op jit(solution)/shard_map/gradient/pallas_call | solution.py:348
  529.8 1.2 copy-done.8
  532.1 2.5 multiply_reduce_fusion.4
  535.9 1.2 multiply_reduce_fusion.3
  537.8 1.4 fusion.18
  539.2 1.3 fusion.17
  542.7 1.2 multiply_reduce_fusion.2
  544.5 2.5 multiply_reduce_fusion.1
  547.7 29.5 %reduce-scatter.17.cloned.1.call-done = bf16[224,2560]{1,0:T(8,128)(2,1)} async-done(((bf16[896,2560]{1,0:T(8,128)(2,1)}), bf16[224,2560]{1,0:T(8,128)(2,1)}) %reduce-scatter.17.cloned.1.call-update) | async-done | bytes 1146896 | tf_op jit(solution)/shard_map/reduce_scatter | solution.py:407
  577.1 2.5 multiply_reduce_fusion
  580.2 1.3 fusion.15
  581.5 9.4 %psum.7 = f32[]{:T(128)} all-reduce(f32[]{:T(128)S(6)} %add.75), channel_id=1, replica_groups=mesh['rep'=4,'dp'=4] {'dp'}, use_global_device_ids=true, to_apply=%region_12.0 | all-reduce | flops 1 | bytes 8 | tf_op jit(solution)/shard_map/psum | solution.py:439
  591.7 1.5 fusion.16
  595.3 8.3 %fusion.8 = (bf16[2,640,896]{2,1,0:T(8,128)(2,1)}, f32[2,640,896]{2,1,0:T(8,128)}, f32[2,640,896]{2,1,0:T(8,128)}) fusion(bf16[2,640,896]{2,1,0:T(8,128)(2,1)S(1)} %copy-done.9, f32[]{:T(128)S(6)} %min_shard_map.3, bf16[1,640,896]{2,1,0:T(8,128)(2,1)S(1)} %bitcast.12, bf16[1,640,896]{2,1,0:T(8,128)(2,1)} %bitcast.13, f32[2,640,896]{2,1,0:T(8,128)} %param.21, ...), kind=kLoop, calls=%fused_computation.17 | loop fusion | flops 22937600 | bytes 25231364 | tf_op jit(solution)/shard_map/convert_element_type | solution.py:395
  603.6 14.7 %fusion.2 = (bf16[2,224,2560]{2,1,0:T(8,128)(2,1)}, f32[2,224,2560]{2,1,0:T(8,128)}, f32[2,224,2560]{2,1,0:T(8,128)}, bf16[2,224,2560]{2,1,0:T(8,128)(2,1)}, f32...) fusion(bf16[2,224,2560]{2,1,0:T(8,128)(2,1)S(1)} %copy-done.1, f32[]{:T(128)S(6)} %min_shard_map.3, ...), kind=kLoop, calls=%fused_computation.11 | loop fusion | flops 45875200 | bytes 50462724 | tf_op jit(solution)/shard_map/convert_element_type | solution.py:395
  (37 shorter events, 6.3 us)
Async XLA Ops:
  7.2 326.6 %reduce-scatter.7.cloned.1.call-start = ((), (), s32[]{:S(2)}) async-start(), calls=%async_computation.6 | async-start | bytes 5734400 | tf_op jit(solution)/shard_map/reduce_scatter | solution.py:407
  7.3 1.6 copy-start
  8.9 1.6 copy-start.2
  54.6 2.1 copy-start.4
  56.7 2.1 copy-start.5
  238.3 179.2 %reduce-scatter.9.cloned.1.call-start = ((), (), s32[]{:S(2)}) async-start(), calls=%async_computation.7 | async-start | bytes 5734400 | tf_op jit(solution)/shard_map/reduce_scatter | solution.py:407
  306.4 167.4 %reduce-scatter.15.cloned.1.call-start = ((), (), s32[]{:S(2)}) async-start(), calls=%async_computation.10 | async-start | bytes 5734400 | tf_op jit(solution)/shard_map/reduce_scatter | solution.py:407
  333.7 169.8 %reduce-scatter.13.cloned.1.call-start = ((), (), s32[]{:S(2)}) async-start(), calls=%async_computation.9 | async-start | bytes 5734400 | tf_op jit(solution)/shard_map/reduce_scatter | solution.py:407
  417.4 127.1 %reduce-scatter.11.cloned.1.call-start = ((), (), s32[]{:S(2)}) async-start(), calls=%async_computation.8 | async-start | bytes 5734400 | tf_op jit(solution)/shard_map/reduce_scatter | solution.py:407
  473.7 103.4 %reduce-scatter.17.cloned.1.call-start = ((), (), s32[]{:S(2)}) async-start(), calls=%async_computation.11 | async-start | bytes 5734400 | tf_op jit(solution)/shard_map/reduce_scatter | solution.py:407
  529.7 1.3 copy-start.8
  529.7 6.2 copy-start.6
  537.7 4.9 copy-start.7
  591.6 3.6 copy-start.9
  595.3 8.3 %copy-start.1 = (bf16[2,224,2560]{2,1,0:T(8,128)(2,1)S(1)}, bf16[2,224,2560]{2,1,0:T(8,128)(2,1)}, u32[]{:S(2)}) copy-start(bf16[2,224,2560]{2,1,0:T(8,128)(2,1)} %refs_1_.4) | copy-start | bytes 6881284
  595.3 8.3 %copy-start.3 = (bf16[2,224,2560]{2,1,0:T(8,128)(2,1)S(1)}, bf16[2,224,2560]{2,1,0:T(8,128)(2,1)}, u32[]{:S(2)}) copy-start(bf16[2,224,2560]{2,1,0:T(8,128)(2,1)} %refs_0_.5) | copy-start | bytes 6881284
Sparse Core Ops, SparseCore 0:
  238.4 47.1 reduce-scatter.6
  306.6 47.1 reduce-scatter.8
  356.7 45.6 reduce-scatter.14
  417.5 47.1 reduce-scatter.12
  473.9 47.1 reduce-scatter.10
  529.9 47.1 reduce-scatter.16

commit v2 on v1

--- a/solution.py
+++ b/solution.py
@@ -34,44 +34,65 @@
 class Gather:
     def __init__(self, n, shards, fulls, stages, local_sem, send_sem, recv_sem):
         self.me, rep = lax.axis_index("dp"), lax.axis_index("rep")
-        self.n, self.p = n, lax.rem(rep, 2)
+        self.n, self.p, self.b = n, lax.rem(rep, 2), lax.rem(rep // 2, 2)
         self.right, self.left = {"dp": lax.rem(self.me + 1, n)}, {"dp": lax.rem(self.me + n - 1, n)}
-        self.partner = {"rep": rep + 1 - 2 * self.p}
+        self.partner, self.sharer = {"rep": rep + 1 - 2 * self.p}, {"rep": rep + 2 - 4 * self.b}
         self.shards, self.fulls, self.stages = shards, fulls, stages
         self.local_sem, self.send_sem, self.recv_sem = local_sem, send_sem, recv_sem
 
     def barrier(self):
         sem = pltpu.get_barrier_semaphore()
-        for device in (self.left, self.right, self.partner):
+        for device in (self.left, self.right, self.partner, self.sharer):
             pl.semaphore_signal(sem, inc=1, device_id=device, device_id_type=MESH)
-        pl.semaphore_wait(sem, 3)
-
-    def half(self, k, away, part=None):
+        pl.semaphore_wait(sem, 4)
+
+    def cut(self, k):
         rows, columns = self.shards[k].shape
+        wide = columns % 256 == 0
+        unit = 128 if wide else 16
+        units = columns // unit if wide else rows // 2 // unit
+        alone = units * 3 // 10
+        return wide, unit, alone, units - 2 * alone
+
+    def place(self, ref, row, k, start, size):
+        wide, unit, _, _ = self.cut(k)
+        if wide:
+            return ref.at[pl.ds(pl.multiple_of(row, 16), self.shards[k].shape[0] // 2), pl.ds(pl.multiple_of(start * unit, unit), size * unit)]
+        return ref.at[pl.ds(pl.multiple_of(row + start * unit, 16), size * unit)]
+
+    def there(self, k, away, start, size):
+        rows = self.shards[k].shape[0]
         owner = lax.rem(self.me + away + self.n, self.n)
-        start = pl.multiple_of(owner * rows + self.p * (rows // 2), 16)
-        if part is None:
-            return self.fulls[k].at[pl.ds(start, rows // 2)]
-        if columns % 256 == 0:
-            return self.fulls[k].at[pl.ds(start, rows // 2), pl.ds(part * (columns // 2), columns // 2)]
-        quarter = rows // 4
-        return self.fulls[k].at[pl.ds(pl.multiple_of(start + part * quarter, 16), quarter)]
+        return self.place(self.fulls[k], owner * rows + self.p * (rows // 2), k, start, size)
 
     def copy(self, k, slot, src, dst, device):
         return pltpu.make_async_remote_copy(src_ref=src, dst_ref=dst, send_sem=self.send_sem.at[k, slot], recv_sem=self.recv_sem.at[k, slot], device_id=device, device_id_type=MESH)
 
     def first(self, k, side):
-        rows = self.shards[k].shape[0]
-        own = self.shards[k].at[pl.ds(pl.multiple_of(self.p * (rows // 2), 16), rows // 2)]
-        return self.copy(k, side, own, self.half(k, 0), self.left if side else self.right)
+        _, _, alone, both = self.cut(k)
+        own = self.place(self.shards[k], self.p * (self.shards[k].shape[0] // 2), k, self.b * alone, alone + both)
+        return self.copy(k, side, own, self.there(k, 0, self.b * alone, alone + both), self.left if side else self.right)
 
     def second(self, k, side):
-        place = self.half(k, 1 if side else -1, side)
+        _, _, alone, both = self.cut(k)
+        size = (alone + both + 1) // 2
+        start = self.b * alone + (size if side else 0)
+        place = self.there(k, 1 if side else -1, start, alone + both - size if side else size)
         return self.copy(k, 2 + side, place, place, self.left if side else self.right)
 
+    def shared(self, k, which):
+        _, _, alone, both = self.cut(k)
+        place = self.there(k, (-1, 1, 2)[which], self.b * (alone + both), alone)
+        return self.copy(k, 4 + which, place, place, self.sharer)
+
     def over(self, k, which):
-        place = self.half(k, (-1, 1, 2)[which])
-        return self.copy(k, 4 + which, place, place, self.partner)
+        _, _, alone, both = self.cut(k)
+        away = (-1, 1, 2)[which % 3]
+        if which < 3:
+            place = self.there(k, away, self.b * alone, alone + both)
+        else:
+            place = self.there(k, away, (1 - self.b) * (alone + both), alone)
+        return self.copy(k, 7 + which, place, place, self.partner)
 
     def load(self, k):
         return pltpu.make_async_copy(self.shards[k], self.stages[k], self.local_sem.at[k, 0])
@@ -94,26 +115,36 @@
         for side in (0, 1):
             self.first(k, side).wait_recv()
             self.second(k, side).start()
-        self.over(k, 0).start()
-        self.over(k, 1).start()
+            self.shared(k, side).start()
+            self.over(k, side).start()
 
     def last(self, k):
         self.second(k, 0).wait_recv()
         self.second(k, 1).wait_recv()
+        self.shared(k, 2).start()
         self.over(k, 2).start()
+        for side in (0, 1):
+            self.shared(k, side).wait_recv()
+            self.over(k, 3 + side).start()
+
+    def end(self, k):
+        self.shared(k, 2).wait_recv()
+        self.over(k, 5).start()
 
     def finish(self, k):
         self.store(k).wait()
-        for which in range(3):
+        for which in range(6):
             self.over(k, which).wait()
         for side in (0, 1):
             self.first(k, side).wait_send()
             self.second(k, side).wait_send()
-
-
-def gather_scratch(weights):
-    k = len(weights)
-    return [pltpu.VMEM(w.shape[1:], w.dtype) for w in weights] + [pltpu.SemaphoreType.DMA((k, 2)), pltpu.SemaphoreType.DMA((k, 7)), pltpu.SemaphoreType.DMA((k, 7))]
+        for which in range(3):
+            self.shared(k, which).wait_send()
+
+
+def gather_scratch(weights, pieces=1):
+    k = len(weights) * pieces
+    return [pltpu.VMEM(w.shape[1:], w.dtype) for w in weights] + [pltpu.SemaphoreType.DMA((k, 2)), pltpu.SemaphoreType.DMA((k, 13)), pltpu.SemaphoreType.DMA((k, 13))]
 
 
 def fulls_of(n, weights):
@@ -122,10 +153,14 @@
 
 def gather_kernel(n, *refs):
     k = (len(refs) - 3) // 3
-    g = Gather(n, [s.at[0] for s in refs[:k]], refs[k : 2 * k], refs[2 * k : 3 * k], *refs[3 * k :])
+    columns = refs[0].shape[2] // 2
+    halves = [pl.ds(half * columns, columns) for half in range(2)]
+    shards = [s.at[0, :, half] for s in refs[:k] for half in halves]
+    fulls, stages = ([s.at[:, half] for s in some for half in halves] for some in (refs[k : 2 * k], refs[2 * k : 3 * k]))
+    g = Gather(n, shards, fulls, stages, *refs[3 * k :])
     g.barrier()
-    for phase in (g.start, g.keep, g.forward, g.last, g.finish):
-        for one in range(k):
+    for phase in (g.start, g.keep, g.forward, g.last, g.end, g.finish):
+        for one in range(2 * k):
             phase(one)
 
 
@@ -137,7 +172,7 @@
         out_shape=fulls_of(n, weights),
         in_specs=[ANY] * k,
         out_specs=[ANY] * k,
-        scratch_shapes=gather_scratch(weights),
+        scratch_shapes=gather_scratch(weights, 2),
         compiler_params=pltpu.CompilerParams(collective_id=0, has_side_effects=True, vmem_limit_bytes=16 * 1024 * 1024),
         cost_estimate=pl.CostEstimate(flops=40_000_000_000, bytes_accessed=8 * sent, transcendentals=0),
         name="gather",
@@ -166,31 +201,23 @@
     return pltpu.CompilerParams(dimension_semantics=("arbitrary",), vmem_limit_bytes=VMEM_LIMIT, **more)
 
 
-def beside(g, k, steps, forwards):
+def beside(g, k, steps, times):
     i = pl.program_id(0)
-
-    @pl.when(i == 0)
-    def _():
-        g.barrier()
-        for one in range(k):
-            g.start(one)
-
-    @pl.when(i == 1)
-    def _():
-        for one in range(k):
-            g.keep(one)
-
-    for one, at in enumerate(forwards):
-
-        @pl.when(i == at)
-        def _(one=one):
-            g.forward(one)
+    phases = (g.start, (0,) * k), (g.keep, (1,) * k), *zip((g.forward, g.last), times)
+    for phase, steps_of in phases:
+        for one, at in enumerate(steps_of):
+
+            @pl.when(i == at)
+            def _(phase=phase, one=one):
+                if phase == g.start and one == 0:
+                    g.barrier()
+                phase(one)
 
 
 def after(g, k, steps):
     @pl.when(pl.program_id(0) == steps - 1)
     def _():
-        for phase in (g.last, g.finish):
+        for phase in (g.end, g.finish):
             for one in range(k):
                 phase(one)
 
@@ -199,7 +226,7 @@
     k = len(layers)
     shards, (gate_ref, up_ref, act_ref, at_ref), refs = refs[:k], refs[k : k + 4], refs[k + 4 :]
     g = Gather(n, [s.at[layer] for s, layer in zip(shards, layers)], refs[:k], refs[k : 2 * k], *refs[2 * k :])
-    beside(g, k, steps, (2, 5))
+    beside(g, k, steps, ((2, 3, 4), (5, 6, 7)))
     a = normed(x_ref[...])
     at_ref[...] = a.T
     for c in range(wg_ref.shape[1] // COLS):
@@ -234,7 +261,7 @@
     k = len(layers)
     shards, (h_ref, at_ref), refs = refs[:k], refs[k : k + 2], refs[k + 2 :]
     g = Gather(n, [s.at[layer] for s, layer in zip(shards, layers)], refs[:k], refs[k : 2 * k], *refs[2 * k :])
-    beside(g, k, steps, (4, 7))
+    beside(g, k, steps, ((3,), (6,)))
     h = x_ref[...] + dot(act_ref[...], wd_ref[...]).astype(BF16)
     h_ref[...] = h
     at_ref[...] = normed(h).T
@@ -357,13 +384,105 @@
     )(at, *ds)
 
 
+LAG = 2
+
+
+def last_kernel(n, counts, at_ref, *refs):
+    k, pieces = len(counts), sum(counts)
+    ds, out_ref, own, moving, send_sem, recv_sem = refs[:k], *refs[k:]
+    i, me = pl.program_id(0), lax.axis_index("dp")
+    right, left = {"dp": lax.rem(me + 1, n)}, {"dp": lax.rem(me + n - 1, n)}
+    rows, cols = own.shape[1] // n, own.shape[2] // 2
+
+    def term(piece, side, hop):
+        block = lax.rem(me + (1 + hop if side else n - 1 - hop), n)
+        return own.at[piece, pl.ds(pl.multiple_of(block * rows, 16), rows), pl.ds(side * cols, cols)]
+
+    def hop_copy(piece, side, hop):
+        src = moving.at[hop - 1, side, piece] if hop else term(piece, side, 0)
+        return pltpu.make_async_remote_copy(src_ref=src, dst_ref=moving.at[hop, side, piece], send_sem=send_sem.at[hop, side, piece], recv_sem=recv_sem.at[hop, side, piece], device_id=left if side else right, device_id_type=MESH)
+
+    @pl.when(i == 0)
+    def _():
+        sem = pltpu.get_barrier_semaphore()
+        for device in (left, right):
+            pl.semaphore_signal(sem, inc=1, device_id=device, device_id_type=MESH)
+        pl.semaphore_wait(sem, 2)
+
+    def at_lag(lag):
+        return jnp.logical_and(i >= lag, i < lag + pieces)
+
+    for hop in range(1, n):
+
+        @pl.when(at_lag(hop * LAG))
+        def _(hop=hop):
+            piece = i - hop * LAG
+            for side in (0, 1):
+                hop_copy(piece, side, hop - 1).wait_recv()
+                total = moving[hop - 1, side, piece].astype(F32) + term(piece, side, hop)[...].astype(F32)
+                if hop < n - 1:
+                    moving[hop - 1, side, piece] = total.astype(BF16)
+                else:
+                    out_ref[:, side * cols : (side + 1) * cols] = total.astype(BF16)
+
+    first = 0
+    for one, count in enumerate(counts):
+
+        @pl.when(jnp.logical_and(i >= first, i < first + count))
+        def _(d_ref=ds[one]):
+            own[i] = dot(at_ref[...], d_ref[...]).astype(BF16)
+
+        first += count
+
+    for hop in range(n - 1):
+
+        @pl.when(at_lag(hop * LAG))
+        def _(hop=hop):
+            for side in (0, 1):
+                hop_copy(i - hop * LAG, side, hop).start()
+
+    @pl.when(at_lag((n - 1) * LAG))
+    def _():
+        for hop in range(n - 1):
+            for side in (0, 1):
+                hop_copy(i - (n - 1) * LAG, side, hop).wait_send()
+
+
+def last_gradient(n, at, ds):
+    (rows, tokens), cols = at.shape, 256
+    counts = [d.shape[1] // cols for d in ds]
+    firsts = [sum(counts[:one]) for one in range(len(ds))]
+    pieces = sum(counts)
+
+    def along(one):
+        return pl.BlockSpec((tokens, cols), lambda i: (0, jnp.clip(i - firsts[one], 0, counts[one] - 1)))
+
+    ff = pieces * cols
+    return pl.pallas_call(
+        functools.partial(last_kernel, n, counts),
+        grid=(pieces + (n - 1) * LAG,),
+        out_shape=jax.ShapeDtypeStruct((rows // n, ff), BF16),
+        in_specs=[whole(at)] + [along(one) for one in range(len(ds))],
+        out_specs=pl.BlockSpec((rows // n, cols), lambda i: (0, jnp.clip(i - (n - 1) * LAG, 0, pieces - 1))),
+        scratch_shapes=[
+            pltpu.VMEM((pieces, rows, cols), BF16),
+            pltpu.VMEM((n - 1, 2, pieces, rows // n, cols // 2), BF16),
+            pltpu.SemaphoreType.DMA((n - 1, 2, pieces)),
+            pltpu.SemaphoreType.DMA((n - 1, 2, pieces)),
+        ],
+        compiler_params=params(collective_id=3, has_side_effects=True),
+        cost_estimate=pl.CostEstimate(flops=4 * tokens * rows * ff, bytes_accessed=2 * (rows * tokens + ff * tokens + rows * ff), transcendentals=0),
+        name="last_gradient",
+    )(at, *ds)
+
+
 def states_kernel(dga_ref, dgb_ref, dua_ref, dub_ref, h_ref, dy_ref, wg_ref, wu_ref, dh_ref, dht_ref):
     ff = dga_ref.shape[1]
 
     def through(a_ref, b_ref, w_ref):
-        return (dot(a_ref[...], w_ref[:, :ff], NT) + dot(b_ref[...], w_ref[:, ff:], NT)).astype(BF16)
-
-    da = (through(dga_ref, dgb_ref, wg_ref) + through(dua_ref, dub_ref, wu_ref)).astype(F32)
+        return (dot(w_ref[:, :ff], a_ref[...], NT) + dot(w_ref[:, ff:], b_ref[...], NT)).astype(BF16)
+
+    da = (through(dga_ref, dgb_ref, wg_ref) + through(dua_ref, dub_ref, wu_ref)).T.astype(F32)
     wide = h_ref[...].astype(F32)
     scale = inv_rms(wide)
     by_scale = jnp.sum(da * wide, -1, keepdims=True)
@@ -388,6 +507,53 @@
     )(*dg, *du, h, dy, full[0], full[1])
 
 
+def clip_kernel(n, count, *refs):
+    sums, (out_ref, parts, send_sem, recv_sem) = refs[:-4], refs[-4:]
+    me = lax.axis_index("dp")
+    others = [{"dp": lax.rem(me + away, n)} for away in range(1, n)]
+    barrier = pltpu.get_barrier_semaphore()
+    for device in others:
+        pl.semaphore_signal(barrier, inc=1, device_id=device, device_id_type=MESH)
+    mine = jnp.zeros((8, 128), F32)
+    for ref in sums:
+        rows, columns = ref.shape
+
+        def more(r, total, ref=ref):
+            wide = ref[pl.ds(pl.multiple_of(r * 16, 16), 16)].astype(F32)
+            return total + wide * wide
+
+        mine = mine + jnp.sum(lax.fori_loop(0, rows // 16, more, jnp.zeros((16, columns), F32)))
+    parts[me] = mine
+    pl.semaphore_wait(barrier, n - 1)
+    copies = [
+        pltpu.make_async_remote_copy(src_ref=parts.at[me], dst_ref=parts.at[me], send_sem=send_sem.at[k], recv_sem=recv_sem.at[k], device_id=device, device_id_type=MESH)
+        for k, device in enumerate(others)
+    ]
+    for copy in copies:
+        copy.start()
+    for copy in copies:
+        copy.wait()
+    total = parts[0]
+    for k in range(1, n):
+        total = total + parts[k]
+    out_ref[...] = jnp.minimum(1.0, 0.5 * lax.rsqrt(total / count + 1e-30))
+
+
+def clip_factor(n, sums):
+    count = n * sum(g.size for g in sums)
+    vmem = pl.BlockSpec(memory_space=pltpu.VMEM)
+    return pl.pallas_call(
+        functools.partial(clip_kernel, n, count),
+        out_shape=jax.ShapeDtypeStruct((8, 128), F32),
+        in_specs=[vmem] * len(sums),
+        out_specs=vmem,
+        scratch_shapes=[pltpu.VMEM((n, 8, 128), F32), pltpu.SemaphoreType.DMA((n - 1,)), pltpu.SemaphoreType.DMA((n - 1,))],
+        compiler_params=pltpu.CompilerParams(collective_id=4, has_side_effects=True, vmem_limit_bytes=32 * 1024 * 1024),
+        cost_estimate=pl.CostEstimate(flops=2 * count, bytes_accessed=2 * count // n, transcendentals=0),
+        name="clip_factor",
+    )(*sums)[0, 0]
+
+
 def adamw(w, m, v, g):
     m = 0.9 * m + 0.1 * g
     v = 0.95 * v + 0.05 * g * g
@@ -395,11 +561,6 @@
     return (w - 0.02 * step).astype(BF16), m, v
 
 
-def clipped(gradients, sum_of_squares, count):
-    factor = jnp.minimum(1.0, 0.5 * lax.rsqrt(sum_of_squares / count + 1e-30))
-    return [g * factor for g in gradients]
-
-
 def solution(mesh):
     n = mesh.shape["dp"]
 
@@ -414,8 +575,8 @@
         x, dy = x[0], dy[0]
         w_gate, w_up, w_down = weights
         full = gathered(n, (w_gate, w_up))
-        gate, up, act, at0, down0, gate1 = up_part(n, x, full, (w_down, w_gate), (0, 1))
-        h, at1, up1, down1 = down_part(n, x, act, down0, (w_up, w_down), (1, 1))
+        gate, up, act, at0, down0, gate1, up1 = up_part(n, x, full, (w_down, w_gate, w_up), (0, 1, 1))
+        h, at1, down1 = down_part(n, x, act, down0, (w_down,), (1,))
         full1 = gate1, up1, down1
 
         act_a, dg_a, du_a = hidden(h, dy, full1, 0)
@@ -433,10 +594,11 @@
         a = gradient(at0, (dg_a, du_a))
         last_a = scattered(a)
         dg_b, du_b = kept_hidden(gate, up, follow(dh, a, sum_down), down0, 1)
-        last_b = scattered(gradient(follow(at0, last_down), (dg_b, du_b)))
+        last_b = last_gradient(n, follow(at0, last_down), (dg_b, du_b))
+        last_a = follow(last_a, last_b)
 
         sums = sum_a, sum_b, sum_down, last_down, last_a, last_b
-        squares = lax.psum(sum(jnp.sum(lax.optimization_barrier(g).astype(F32) ** 2) for g in sums), "dp")
+        factor = clip_factor(n, sums)
 
         def joined(a, b, side):
             half = a.shape[1] // 2
@@ -445,7 +607,7 @@
         pairs = (last_a, last_b), (sum_a, sum_b)
         gradients = [jnp.stack([joined(a, b, side) for a, b in pairs]).astype(F32) for side in range(2)]
         gradients.append(jnp.stack([last_down, sum_down]).astype(F32))
-        gradients = clipped(gradients, squares, lax.psum(1, "dp") * sum(g.size for g in gradients))
+        gradients = [g * factor for g in gradients]
         new = [adamw(w.astype(F32), m, v, g) for w, m, v, g in zip(weights, m, v, gradients, strict=True)]
         return tuple(one[which] for which in range(3) for one in new)
 

time: 634 us -> 603 us (0.951)
  waiting for transfers between devices: 29.9 us -> 0.33 us
  Pallas kernels: 514 us -> 535 us
  other arithmetic: 38.3 us -> 28.7 us
  blocking collectives: 9.41 us -> 0 us
    pallas_call x0 -> x2, Pallas kernels: none -> 66.1 us  [the longest x1 59.4 us: last_gradient(): pl.pallas_call(functools.partial(last_kernel, n, counts), grid=(pieces +...]
    reduce_scatter x6 -> x5, waiting for transfers between devices: 29.5 us -> 0.06 us  [scattered(): return lax.psum_scatter(g, 'dp', scatter_dimension=0, tiled=True)]
    pallas_call x6 -> x5, Pallas kernels: 158 us -> 132 us  [gradient(): pl.pallas_call(functools.partial(gradient_kernel, turn, counts), grid=(su...]
    pallas_call x1, Pallas kernels: 47.6 us -> 35.3 us  [down_part(): pl.pallas_call(functools.partial(down_kernel, n, layers, steps), grid=(st...]
    reduce_sum x6 -> x0, other arithmetic: 10.9 us -> none  [step(): jnp.sum(lax.optimization_barrier(g).astype(F32) ** 2)]
    psum x1 -> x0, blocking collectives: 9.41 us -> none  [step(): lax.psum(sum((jnp.sum(lax.optimization_barrier(g).astype(F32) ** 2) for g...]
    unnamed x20 -> x32, local copies, waits for them, and re-layouts: 8.78 us -> 12.8 us
  transfers between devices with their start and end apart: 6 -> 5, of which waited for: 1 -> 0; matrix products, arithmetic and copies ran while one was open for 2% -> 1% of each run, Pallas kernels for 46% -> 54%
where the time goes in v2:
time: 603 us; the launch traced here: 596 us
  Pallas kernels  535 us (89%)
  other arithmetic  28.7 us (5%)
  local copies, waits for them, and re-layouts  17.3 us (3%)
  between operations  14.2 us (2%)
    pallas_call x5, Pallas kernels, gradient(): pl.pallas_call(functools.partial(gradient_kernel, turn, counts), grid=(su...  132 us
    pallas_call x2, Pallas kernels, hidden(): pl.pallas_call(hidden_kernel, grid=(tokens // ROWS,), out_shape=[wide] *...  83.8 us
    pallas_call x1, Pallas kernels, up_part(): pl.pallas_call(functools.partial(up_kernel, n, layers, steps), grid=(step...  65.6 us
    pallas_call x2, Pallas kernels, kept_hidden(): pl.pallas_call(kept_kernel, grid=(tokens // ROWS,), out_shape=[wide] * 2,...  59.5 us
    pallas_call x1, Pallas kernels, last_gradient(): pl.pallas_call(functools.partial(last_kernel, n, counts), grid=(pieces +...  59.4 us
    pallas_call x1, Pallas kernels, states(): pl.pallas_call(states_kernel, grid=(tokens // ROWS,), out_shape=[jax.Shap...  54.1 us
    pallas_call x1, Pallas kernels, gathered(): pl.pallas_call(functools.partial(gather_kernel, n), out_shape=fulls_of(n,...  39.1 us
    pallas_call x1, Pallas kernels, down_part(): pl.pallas_call(functools.partial(down_kernel, n, layers, steps), grid=(st...  35.3 us
  transfers between devices with their start and end apart: 5, of which 0 were waited for; matrix products, arithmetic and copies ran while one was open for 1% of the time, Pallas kernels for 54%

profile of v2, /device:TPU:112, one launch (start us, length us, event | category | flops | bytes accessed | tf_op | source)
XLA Modules:
  0.0 595.9 jit_solution(6864837466753707639)
XLA Ops:
  7.3 1.6 copy-done.7
  8.9 1.6 copy-done.9
  10.6 39.1 %gather.1 = (bf16[896,2560]{1,0:T(8,128)(2,1)S(1)}, bf16[896,2560]{1,0:T(8,128)(2,1)S(1)}) custom-call(bf16[2,224,2560]{2,1,0:T(8,128)(2,1)S(1)} %copy-done.7, bf16[2,224,2560]{2,1,0:T(8,128)(2,1)S(1)} %copy-done.9), custom_call_target="tpu_custom_call" | custom-call | flops 40000000000 | bytes 27525120 | tf_op jit(solution)/shard_map/gather/pallas_call | solution.py:170
  49.6 2.1 copy-done.10
  51.8 2.1 copy-done.11
  53.9 65.6 %up.1 = (f32[4096,2560]{1,0:T(8,128)}, f32[4096,2560]{1,0:T(8,128)}, bf16[4096,2560]{1,0:T(8,128)(2,1)}, bf16[896,4096]{1,0:T(8,128)(2,1)}, bf16[2560,896]{1,0:T...) custom-call(bf16[4096,896]{1,0:T(8,128)(2,1)} %bitcast.15, bf16[896,2560]{1,0:T(8,128)(2,1)} %copy-done.10, ...), custom_call_target="tpu_custom_call" | custom-call | flops 37580963840 | bytes 104857600 | tf_op jit(solution)/shard_map/up/pallas_call | solution.py:247
  119.5 35.3 %down.1 = (bf16[4096,896]{1,0:T(8,128)(2,1)}, bf16[896,4096]{1,0:T(8,128)(2,1)}, bf16[2560,896]{1,0:T(8,128)(2,1)}) custom-call(bf16[4096,896]{1,0:T(8,128)(2,1)} %bitcast.16, bf16[4096,2560]{1,0:T(8,128)(2,1)} %get-tuple-element.46.act_ref.refs_0_, bf16[2560,896]{1,0:T(8,128)(2,1)} %get-tuple-element.47.wd_ref, bf16[2,640,896]{2,1,0:T(8,128)(2,1)} %refs_0_.5), custom_call_target="tpu_custom_call" | custom-call | flops 18790481920 | bytes 42991616 | tf_op jit(solution)/shard_map/down/pallas_call | solution.py:275
  154.8 41.7 %hidden.2 = (bf16[4096,1280]{1,0:T(8,128)(2,1)}, bf16[4096,1280]{1,0:T(8,128)(2,1)}, bf16[4096,1280]{1,0:T(8,128)(2,1)}) custom-call(bf16[4096,896]{1,0:T(8,128)(2,1)} %get-tuple-element.62.h_ref, bf16[4096,896]{1,0:T(8,128)(2,1)} %bitcast.17, bf16[896,2560]{1,0:T(8,128)(2,1)} %get-tuple-element.49.wg_ref, bf16[896,2560]{1,0:T(8,128)(2,1)} %get-tuple-element.50.wu_ref, ...), custom_call_target="tpu_custom_call" | custom-call | flops 28185722880 | bytes 53018624 | tf_op jit(solution)/shard_map/hidden/pallas_call | solution.py:311
  196.5 26.2 %gradient.5 = bf16[896,2560]{1,0:T(8,128)(2,1)} custom-call(bf16[896,4096]{1,0:T(8,128)(2,1)} %get-tuple-element.53.at_ref, bf16[4096,1280]{1,0:T(8,128)(2,1)} %get-tuple-element.52.refs_0_.dga_ref, bf16[4096,1280]{1,0:T(8,128)(2,1)} %get-tuple-element.54.refs_1_.dua_ref), custom_call_target="tpu_custom_call" | custom-call | flops 18790481920 | bytes 32899072 | tf_op jit(solution)/shard_map/gradient/pallas_call | solution.py:375
  222.8 42.1 %hidden.3 = (bf16[4096,1280]{1,0:T(8,128)(2,1)}, bf16[4096,1280]{1,0:T(8,128)(2,1)}, bf16[4096,1280]{1,0:T(8,128)(2,1)}, bf16[896,4096]{1,0:T(8,128)(2,1)}) custom-call(bf16[4096,896]{1,0:T(8,128)(2,1)} %get-tuple-element.62.h_ref, bf16[4096,896]{1,0:T(8,128)(2,1)} %bitcast.18, bf16[896,2560]{1,0:T(8,128)(2,1)} %get-tuple-element.49.wg_ref, ...), custom_call_target="tpu_custom_call" | custom-call | flops 28185722880 | bytes 53018624 | tf_op jit(solution)/shard_map/hidden/pallas_call | solution.py:311
  265.0 26.2 %gradient.6 = bf16[896,2560]{1,0:T(8,128)(2,1)} custom-call(bf16[896,4096]{1,0:T(8,128)(2,1)} %get-tuple-element.53.at_ref, bf16[4096,1280]{1,0:T(8,128)(2,1)} %get-tuple-element.56.refs_0_.dgb_ref, bf16[4096,1280]{1,0:T(8,128)(2,1)} %get-tuple-element.57.refs_1_.dub_ref), custom_call_target="tpu_custom_call" | custom-call | flops 18790481920 | bytes 32899072 | tf_op jit(solution)/shard_map/gradient/pallas_call | solution.py:375
  291.3 26.9 %gradient.7 = bf16[2560,896]{1,0:T(8,128)(2,1)} custom-call(bf16[896,4096]{1,0:T(8,128)(2,1)} %get-tuple-element.59.at_ref, bf16[4096,1280]{1,0:T(8,128)(2,1)} %get-tuple-element.60.refs_0_, bf16[4096,1280]{1,0:T(8,128)(2,1)} %get-tuple-element.61.refs_1_), custom_call_target="tpu_custom_call" | custom-call | flops 18790481920 | bytes 32899072 | tf_op jit(solution)/shard_map/gradient/pallas_call | solution.py:375
  318.4 54.1 %states.1 = (bf16[4096,896]{1,0:T(8,128)(2,1)}, bf16[896,4096]{1,0:T(8,128)(2,1)}) custom-call(bf16[4096,1280]{1,0:T(8,128)(2,1)} %get-tuple-element.52.refs_0_.dga_ref, bf16[4096,1280]{1,0:T(8,128)(2,1)} %get-tuple-element.56.refs_0_.dgb_ref, bf16[4096,1280]{1,0:T(8,128)(2,1)} %get-tuple-element.54.refs_1_.dua_ref, ...), custom_call_target="tpu_custom_call" | custom-call | flops 37580963840 | bytes 80478208 | tf_op jit(solution)/shard_map/states/pallas_call | solution.py:498
  372.5 26.1 %gradient.8 = bf16[2560,896]{1,0:T(8,128)(2,1)} custom-call(bf16[896,4096]{1,0:T(8,128)(2,1)} %get-tuple-element.64.at_ref, bf16[4096,2560]{1,0:T(8,128)(2,1)} %get-tuple-element.46.act_ref.refs_0_), custom_call_target="tpu_custom_call" | custom-call | flops 18790481920 | bytes 32899072 | tf_op jit(solution)/shard_map/gradient/pallas_call | solution.py:375
  398.7 29.7 %kept_hidden.2 = (bf16[4096,1280]{1,0:T(8,128)(2,1)}, bf16[4096,1280]{1,0:T(8,128)(2,1)}) custom-call(f32[4096,2560]{1,0:T(8,128)} %get-tuple-element.44.gate_ref, f32[4096,2560]{1,0:T(8,128)} %get-tuple-element.45.up_ref, bf16[4096,896]{1,0:T(8,128)(2,1)} %get-tuple-element.69.dy_ref, bf16[2560,896]{1,0:T(8,128)(2,1)} %get-tuple-element.47.wd_ref), custom_call_target="tpu_custom_call" | custom-call | flops 9395240960 | bytes 72548352 | tf_op jit(solution)/shard_map/kept_hidden/pallas_call | solution.py:337
  428.4 26.2 %gradient.9 = bf16[896,2560]{1,0:T(8,128)(2,1)} custom-call(bf16[896,4096]{1,0:T(8,128)(2,1)} %get-tuple-element.68.at_ref, bf16[4096,1280]{1,0:T(8,128)(2,1)} %get-tuple-element.66.refs_0_, bf16[4096,1280]{1,0:T(8,128)(2,1)} %get-tuple-element.67.refs_1_), custom_call_target="tpu_custom_call" | custom-call | flops 18790481920 | bytes 32899072 | tf_op jit(solution)/shard_map/gradient/pallas_call | solution.py:375
  454.7 1.2 copy-done.3
  456.3 1.1 maximum_bitcast_fusion.1
  457.4 1.1 maximum_bitcast_fusion.3
  458.5 29.8 %kept_hidden.3 = (bf16[4096,1280]{1,0:T(8,128)(2,1)}, bf16[4096,1280]{1,0:T(8,128)(2,1)}) custom-call(f32[4096,2560]{1,0:T(8,128)} %get-tuple-element.44.gate_ref, f32[4096,2560]{1,0:T(8,128)} %get-tuple-element.45.up_ref, bf16[4096,896]{1,0:T(8,128)(2,1)} %get-tuple-element.69.dy_ref, bf16[2560,896]{1,0:T(8,128)(2,1)} %get-tuple-element.47.wd_ref), custom_call_target="tpu_custom_call" | custom-call | flops 9395240960 | bytes 72548352 | tf_op jit(solution)/shard_map/kept_hidden/pallas_call | solution.py:337
  488.2 59.4 %last_gradient.1.refs_5_ = bf16[224,2560]{1,0:T(8,128)(2,1)} custom-call(bf16[896,4096]{1,0:T(8,128)(2,1)} %get-tuple-element.68.at_ref, bf16[4096,1280]{1,0:T(8,128)(2,1)} %get-tuple-element.70.refs_0_, bf16[4096,1280]{1,0:T(8,128)(2,1)} %get-tuple-element.71.refs_1_), custom_call_target="tpu_custom_call" | custom-call | flops 37580963840 | bytes 32899072 | tf_op jit(solution)/shard_map/last_gradient/pallas_call | solution.py:461
  547.6 2.5 fusion.16
  550.1 1.4 fusion.15
  551.5 1.2 copy-done.4
  552.7 1.3 copy-done.5
  554.0 1.3 copy-done.6
  555.2 6.8 %clip_factor.1 = f32[8,128]{1,0:T(8,128)S(1)} custom-call(bf16[224,2560]{1,0:T(8,128)(2,1)S(1)} %copy-done.2, bf16[224,2560]{1,0:T(8,128)(2,1)S(1)} %copy-done.4, bf16[640,896]{1,0:T(8,128)(2,1)S(1)} %copy-done, bf16[640,896]{1,0:T(8,128)(2,1)S(1)} %copy-done.1, bf16[224,2560]{1,0:T(8,128)(2,1)S(1)} %copy-done.5, bf16[224,2560]{1,0:T(8,128)(2,1)S(1)} %copy-done.6), custom_call_target="tpu_custom_call" | custom-call | flops 27525120 | bytes 6881280 | tf_op jit(solution)/shard_map/clip_factor/pallas_call | solution.py:545
  562.0 0.5 slice.31
  562.5 1.1 maximum_bitcast_fusion
  563.6 1.1 maximum_bitcast_fusion.2
  564.7 9.0 %fusion.8 = (bf16[2,640,896]{2,1,0:T(8,128)(2,1)}, f32[2,640,896]{2,1,0:T(8,128)}, f32[2,640,896]{2,1,0:T(8,128)}) fusion(bf16[2,640,896]{2,1,0:T(8,128)(2,1)S(1)} %copy-done.15, f32[]{:T(128)} %bitcast.4, bf16[1,640,896]{2,1,0:T(8,128)(2,1)S(1)} %bitcast.13, bf16[1,640,896]{2,1,0:T(8,128)(2,1)S(1)} %bitcast.14, f32[2,640,896]{2,1,0:T(8,128)} %param.21, ...), kind=kLoop, calls=%fused_computation.17 | loop fusion | flops 22937600 | bytes 25231364 | tf_op jit(solution)/shard_map/convert_element_type | solution.py:561
  573.7 15.4 %fusion.2 = (bf16[2,224,2560]{2,1,0:T(8,128)(2,1)}, f32[2,224,2560]{2,1,0:T(8,128)}, f32[2,224,2560]{2,1,0:T(8,128)}, bf16[2,224,2560]{2,1,0:T(8,128)(2,1)}, f32...) fusion(bf16[2,224,2560]{2,1,0:T(8,128)(2,1)S(1)} %copy-done.8, f32[]{:T(128)} %bitcast.4, ...), kind=kLoop, calls=%fused_computation.11 | loop fusion | flops 45875200 | bytes 50462724 | tf_op jit(solution)/shard_map/convert_element_type | solution.py:561
  (41 shorter events, 1.1 us)
Async XLA Ops:
  7.2 311.2 %reduce-scatter.6.cloned.1.call-start = ((), (), s32[]{:S(2)}) async-start(), calls=%async_computation.5 | async-start | bytes 5734400 | tf_op jit(solution)/shard_map/reduce_scatter | solution.py:568
  7.3 1.6 copy-start.7
  8.9 1.6 copy-start.9
  49.6 2.1 copy-start.10
  51.8 2.1 copy-start.11
  222.8 175.9 %reduce-scatter.8.cloned.1.call-start = ((), (), s32[]{:S(2)}) async-start(), calls=%async_computation.6 | async-start | bytes 5734400 | tf_op jit(solution)/shard_map/reduce_scatter | solution.py:568
  291.2 163.5 %reduce-scatter.14.cloned.1.call-start = ((), (), s32[]{:S(2)}) async-start(), calls=%async_computation.9 | async-start | bytes 5734400 | tf_op jit(solution)/shard_map/reduce_scatter | solution.py:568
  318.3 169.9 %reduce-scatter.12.cloned.1.call-start = ((), (), s32[]{:S(2)}) async-start(), calls=%async_computation.8 | async-start | bytes 5734400 | tf_op jit(solution)/shard_map/reduce_scatter | solution.py:568
  398.6 151.5 %reduce-scatter.10.cloned.1.call-start = ((), (), s32[]{:S(2)}) async-start(), calls=%async_computation.7 | async-start | bytes 5734400 | tf_op jit(solution)/shard_map/reduce_scatter | solution.py:568
  454.6 1.3 copy-start.3
  454.6 1.6 copy-start.2
  547.6 3.9 copy-start
  547.6 3.9 copy-start.1
  550.1 12.5 %copy-start.14 = (bf16[224,1280]{1,0:T(8,128)(2,1)S(1)}, bf16[224,1280]{1,0:T(8,128)(2,1)}, u32[]{:S(2)}) copy-start(bf16[224,1280]{1,0:T(8,128)(2,1)} %get-tuple-element.85) | copy-start | bytes 1720324
  551.5 1.3 copy-start.4
  552.7 1.3 copy-start.5
  554.0 1.3 copy-start.6
  555.2 8.4 %copy-start.13 = (bf16[224,1280]{1,0:T(8,128)(2,1)S(1)}, bf16[224,1280]{1,0:T(8,128)(2,1)}, u32[]{:S(2)}) copy-start(bf16[224,1280]{1,0:T(8,128)(2,1)} %get-tuple-element.84) | copy-start | bytes 1720324
  555.2 9.5 %copy-start.15 = (bf16[2,640,896]{2,1,0:T(8,128)(2,1)S(1)}, bf16[2,640,896]{2,1,0:T(8,128)(2,1)}, u32[]{:S(2)}) copy-start(bf16[2,640,896]{2,1,0:T(8,128)(2,1)} %refs_0_.5) | copy-start | bytes 6881284
  564.7 9.0 %copy-start.8 = (bf16[2,224,2560]{2,1,0:T(8,128)(2,1)S(1)}, bf16[2,224,2560]{2,1,0:T(8,128)(2,1)}, u32[]{:S(2)}) copy-start(bf16[2,224,2560]{2,1,0:T(8,128)(2,1)} %refs_1_.3) | copy-start | bytes 6881284
  564.7 9.0 %copy-start.12 = (bf16[1,224,2560]{2,1,0:T(8,128)(2,1)S(1)}, bf16[1,224,2560]{2,1,0:T(8,128)(2,1)}, u32[]{:S(2)}) copy-start(bf16[1,224,2560]{2,1,0:T(8,128)(2,1)} %maximum_bitcast_fusion.1) | copy-start | bytes 3440644
Sparse Core Ops, SparseCore 0:
  222.9 45.2 reduce-scatter.5
  291.4 45.2 reduce-scatter.7
  339.5 45.6 reduce-scatter.13
  398.7 45.2 reduce-scatter.11
  454.8 45.2 reduce-scatter.9

commit v3 on v2

--- a/solution.py
+++ b/solution.py
@@ -13,6 +13,7 @@
 VMEM_LIMIT = 60 * 1024 * 1024
 ROWS = 512
 COLS = 256
+EARLY = 1024
 
 
 def dot(a, b, dims=((1,), (0,))):
@@ -173,7 +174,7 @@
         in_specs=[ANY] * k,
         out_specs=[ANY] * k,
         scratch_shapes=gather_scratch(weights, 2),
-        compiler_params=pltpu.CompilerParams(collective_id=0, has_side_effects=True, vmem_limit_bytes=16 * 1024 * 1024),
+        compiler_params=pltpu.CompilerParams(collective_id=0, has_side_effects=True, vmem_limit_bytes=VMEM_LIMIT),
         cost_estimate=pl.CostEstimate(flops=40_000_000_000, bytes_accessed=8 * sent, transcendentals=0),
         name="gather",
     )(*weights)
@@ -224,7 +225,7 @@
 
 def up_kernel(n, layers, steps, x_ref, wg_ref, wu_ref, *refs):
     k = len(layers)
-    shards, (gate_ref, up_ref, act_ref, at_ref), refs = refs[:k], refs[k : k + 4], refs[k + 4 :]
+    shards, (*kept, act_ref, at_ref), refs = refs[:k], refs[k : k + 6], refs[k + 6 :]
     g = Gather(n, [s.at[layer] for s, layer in zip(shards, layers)], refs[:k], refs[k : 2 * k], *refs[2 * k :])
     beside(g, k, steps, ((2, 3, 4), (5, 6, 7)))
     a = normed(x_ref[...])
@@ -233,8 +234,10 @@
         cols = pl.ds(c * COLS, COLS)
         gate = dot(a, wg_ref[:, cols])
         up = dot(a, wu_ref[:, cols])
-        gate_ref[:, cols] = gate
-        up_ref[:, cols] = up
+        late = c * COLS >= EARLY
+        there = pl.ds(c * COLS - EARLY * late, COLS)
+        kept[late][:, there] = gate
+        kept[2 + late][:, there] = up
         act_ref[:, cols] = (gate * jax.nn.sigmoid(gate) * up).astype(BF16)
     after(g, k, steps)
 
@@ -243,13 +246,13 @@
     tokens, d = x.shape
     ff, k = full[0].shape[1], len(weights)
     steps = tokens // ROWS
-    wide = jax.ShapeDtypeStruct((tokens, ff), F32)
+    widths = (EARLY, ff - EARLY) * 2
     return pl.pallas_call(
         functools.partial(up_kernel, n, layers, steps),
         grid=(steps,),
-        out_shape=[wide, wide, jax.ShapeDtypeStruct((tokens, ff), BF16), jax.ShapeDtypeStruct((d, tokens), BF16), *fulls_of(n, weights)],
+        out_shape=[*(jax.ShapeDtypeStruct((tokens, width), F32) for width in widths), jax.ShapeDtypeStruct((tokens, ff), BF16), jax.ShapeDtypeStruct((d, tokens), BF16), *fulls_of(n, weights)],
         in_specs=[rows_of(d), whole(full[0]), whole(full[1])] + [ANY] * k,
-        out_specs=[rows_of(ff)] * 3 + [columns_of(d)] + [ANY] * k,
+        out_specs=[*(rows_of(width) for width in widths), rows_of(ff), columns_of(d)] + [ANY] * k,
         scratch_shapes=gather_scratch(weights),
         compiler_params=params(collective_id=1, has_side_effects=True),
         cost_estimate=pl.CostEstimate(flops=4 * tokens * d * ff, bytes_accessed=10 * tokens * ff, transcendentals=tokens * ff),
@@ -320,25 +323,24 @@
     )(h, dy, *full)
 
 
-def kept_kernel(gate_ref, up_ref, dy_ref, wd_ref, dg_ref, du_ref):
+def kept_kernel(start, gate_ref, up_ref, dy_ref, wd_ref, dg_ref, du_ref):
     dy = dy_ref[...]
     for c in range(gate_ref.shape[1] // COLS):
         cols = pl.ds(c * COLS, COLS)
         gate = gate_ref[:, cols]
-        dact = dot(dy, wd_ref[cols, :], NT).astype(BF16).astype(F32)
+        dact = dot(dy, wd_ref[pl.ds(start + c * COLS, COLS), :], NT).astype(BF16).astype(F32)
         dg_ref[:, cols], du_ref[:, cols] = by_hidden(gate, up_ref[:, cols], dact, jax.nn.sigmoid(gate))
 
 
-def kept_hidden(gate, up, dy, full, half):
+def kept_hidden(gate, up, dy, full, start):
     tokens, d = dy.shape
-    ff = gate.shape[1] // 2
+    ff = gate.shape[1]
     wide = jax.ShapeDtypeStruct((tokens, ff), BF16)
-    block = pl.BlockSpec((ROWS, ff), lambda i: (i, half))
-    return pl.pallas_call(
-        kept_kernel,
+    return pl.pallas_call(
+        functools.partial(kept_kernel, start),
         grid=(tokens // ROWS,),
         out_shape=[wide] * 2,
-        in_specs=[block, block, rows_of(d), part_of(full, 0, half)],
+        in_specs=[rows_of(ff), rows_of(ff), rows_of(d), whole(full)],
         out_specs=[rows_of(ff)] * 2,
         compiler_params=params(),
         cost_estimate=pl.CostEstimate(flops=2 * tokens * d * ff, bytes_accessed=2 * tokens * d + 12 * tokens * ff + 2 * d * ff, transcendentals=tokens * ff),
@@ -575,7 +577,7 @@
         x, dy = x[0], dy[0]
         w_gate, w_up, w_down = weights
         full = gathered(n, (w_gate, w_up))
-        gate, up, act, at0, down0, gate1, up1 = up_part(n, x, full, (w_down, w_gate, w_up), (0, 1, 1))
+        gate_a, gate_b, up_a, up_b, act, at0, down0, gate1, up1 = up_part(n, x, full, (w_down, w_gate, w_up), (0, 1, 1))
         h, at1, down1 = down_part(n, x, act, down0, (w_down,), (1,))
         full1 = gate1, up1, down1
 
@@ -590,10 +592,10 @@
         dh, dht = states((dg_a, dg_b), (du_a, du_b), follow(h, one_down, sum_a), dy, full1)
         down = gradient(dht, (act,), True)
         last_down = scattered(down)
-        dg_a, du_a = kept_hidden(gate, up, follow(dh, down, sum_b), down0, 0)
+        dg_a, du_a = kept_hidden(gate_a, up_a, follow(dh, down, sum_b), down0, 0)
         a = gradient(at0, (dg_a, du_a))
         last_a = scattered(a)
-        dg_b, du_b = kept_hidden(gate, up, follow(dh, a, sum_down), down0, 1)
+        dg_b, du_b = kept_hidden(gate_b, up_b, follow(dh, a, sum_down), down0, EARLY)
         last_b = last_gradient(n, follow(at0, last_down), (dg_b, du_b))
         last_a = follow(last_a, last_b)
 
@@ -601,8 +603,7 @@
         factor = clip_factor(n, sums)
 
         def joined(a, b, side):
-            half = a.shape[1] // 2
-            return jnp.concatenate([one[:, side * half : (side + 1) * half] for one in (a, b)], -1)
+            return jnp.concatenate([jnp.split(one, 2, -1)[side] for one in (a, b)], -1)
 
         pairs = (last_a, last_b), (sum_a, sum_b)
         gradients = [jnp.stack([joined(a, b, side) for a, b in pairs]).astype(F32) for side in range(2)]

time: 603 us -> 605 us (level)
  Pallas kernels: 535 us -> 543 us
  local copies, waits for them, and re-layouts: 17.3 us -> 10.4 us
    pallas_call x1, Pallas kernels: 59.4 us -> 66.9 us  [last_gradient(): pl.pallas_call(functools.partial(last_kernel, n, counts), grid=(pieces +...]
    unnamed x32 -> x26, local copies, waits for them, and re-layouts: 12.8 us -> 6.06 us
  transfers between devices with their start and end apart: 5 -> 5, of which waited for: 0 -> 0; matrix products, arithmetic and copies ran while one was open for 1% -> 1% of each run, Pallas kernels for 54% -> 55%
where the time goes in v3:
time: 605 us; the launch traced here: 595 us
  Pallas kernels  543 us (90%)
  other arithmetic  26.7 us (4%)
  between operations  14.5 us (2%)
  local copies, waits for them, and re-layouts  10.4 us (2%)
    pallas_call x5, Pallas kernels, gradient(): pl.pallas_call(functools.partial(gradient_kernel, turn, counts), grid=(su...  128 us
    pallas_call x2, Pallas kernels, hidden(): pl.pallas_call(hidden_kernel, grid=(tokens // ROWS,), out_shape=[wide] *...  83.4 us
    pallas_call x1, Pallas kernels, last_gradient(): pl.pallas_call(functools.partial(last_kernel, n, counts), grid=(pieces +...  66.9 us
    pallas_call x1, Pallas kernels, up_part(): pl.pallas_call(functools.partial(up_kernel, n, layers, steps), grid=(step...  65.7 us
    pallas_call x2, Pallas kernels, kept_hidden(): pl.pallas_call(functools.partial(kept_kernel, start), grid=(tokens // ROW...  63.3 us
    pallas_call x1, Pallas kernels, states(): pl.pallas_call(states_kernel, grid=(tokens // ROWS,), out_shape=[jax.Shap...  53.7 us
    pallas_call x1, Pallas kernels, gathered(): pl.pallas_call(functools.partial(gather_kernel, n), out_shape=fulls_of(n,...  39.1 us
    pallas_call x1, Pallas kernels, down_part(): pl.pallas_call(functools.partial(down_kernel, n, layers, steps), grid=(st...  35.3 us
  transfers between devices with their start and end apart: 5, of which 0 were waited for; matrix products, arithmetic and copies ran while one was open for 1% of the time, Pallas kernels for 55%

profile of v3, /device:TPU:112, one launch (start us, length us, event | category | flops | bytes accessed | tf_op | source)
XLA Modules:
  0.0 595.2 jit_solution(10205968051171752366)
XLA Ops:
  7.3 39.1 %gather.1 = (bf16[896,2560]{1,0:T(8,128)(2,1)}, bf16[896,2560]{1,0:T(8,128)(2,1)}) custom-call(bf16[2,224,2560]{2,1,0:T(8,128)(2,1)} %refs_1_.3, bf16[2,224,2560]{2,1,0:T(8,128)(2,1)} %refs_2_.1), custom_call_target="tpu_custom_call" | custom-call | flops 40000000000 | bytes 27525120 | tf_op jit(solution)/shard_map/gather/pallas_call | solution.py:171
  46.4 65.7 %up.1 = (f32[4096,1024]{1,0:T(8,128)}, f32[4096,1536]{1,0:T(8,128)}, f32[4096,1024]{1,0:T(8,128)}, f32[4096,1536]{1,0:T(8,128)}, bf16[4096,2560]{1,0:T(8,128)(2,...) custom-call(bf16[4096,896]{1,0:T(8,128)(2,1)} %bitcast.15, ...), custom_call_target="tpu_custom_call" | custom-call | flops 37580963840 | bytes 104857600 | tf_op jit(solution)/shard_map/up/pallas_call | solution.py:250
  112.1 35.3 %down.1 = (bf16[4096,896]{1,0:T(8,128)(2,1)}, bf16[896,4096]{1,0:T(8,128)(2,1)}, bf16[2560,896]{1,0:T(8,128)(2,1)}) custom-call(bf16[4096,896]{1,0:T(8,128)(2,1)} %bitcast.16, bf16[4096,2560]{1,0:T(8,128)(2,1)} %get-tuple-element.48.act_ref.refs_0_, bf16[2560,896]{1,0:T(8,128)(2,1)} %get-tuple-element.49.wd_ref, bf16[2,640,896]{2,1,0:T(8,128)(2,1)} %refs_0_.5), custom_call_target="tpu_custom_call" | custom-call | flops 18790481920 | bytes 42991616 | tf_op jit(solution)/shard_map/down/pallas_call | solution.py:278
  147.4 41.5 %hidden.2 = (bf16[4096,1280]{1,0:T(8,128)(2,1)}, bf16[4096,1280]{1,0:T(8,128)(2,1)}, bf16[4096,1280]{1,0:T(8,128)(2,1)}) custom-call(bf16[4096,896]{1,0:T(8,128)(2,1)} %get-tuple-element.64.h_ref, bf16[4096,896]{1,0:T(8,128)(2,1)} %bitcast.17, bf16[896,2560]{1,0:T(8,128)(2,1)} %get-tuple-element.51.wg_ref, bf16[896,2560]{1,0:T(8,128)(2,1)} %get-tuple-element.52.wu_ref, ...), custom_call_target="tpu_custom_call" | custom-call | flops 28185722880 | bytes 53018624 | tf_op jit(solution)/shard_map/hidden/pallas_call | solution.py:314
  188.9 26.4 %gradient.5 = bf16[896,2560]{1,0:T(8,128)(2,1)} custom-call(bf16[896,4096]{1,0:T(8,128)(2,1)} %get-tuple-element.55.at_ref, bf16[4096,1280]{1,0:T(8,128)(2,1)} %get-tuple-element.54.refs_0_.dga_ref, bf16[4096,1280]{1,0:T(8,128)(2,1)} %get-tuple-element.56.refs_1_.dua_ref), custom_call_target="tpu_custom_call" | custom-call | flops 18790481920 | bytes 32899072 | tf_op jit(solution)/shard_map/gradient/pallas_call | solution.py:377
  215.3 0.1 reduce-scatter.8.cloned.1.call-start
  215.4 41.9 %hidden.3 = (bf16[4096,1280]{1,0:T(8,128)(2,1)}, bf16[4096,1280]{1,0:T(8,128)(2,1)}, bf16[4096,1280]{1,0:T(8,128)(2,1)}, bf16[896,4096]{1,0:T(8,128)(2,1)}) custom-call(bf16[4096,896]{1,0:T(8,128)(2,1)} %get-tuple-element.64.h_ref, bf16[4096,896]{1,0:T(8,128)(2,1)} %bitcast.18, bf16[896,2560]{1,0:T(8,128)(2,1)} %get-tuple-element.51.wg_ref, ...), custom_call_target="tpu_custom_call" | custom-call | flops 28185722880 | bytes 53018624 | tf_op jit(solution)/shard_map/hidden/pallas_call | solution.py:314
  257.3 26.2 %gradient.6 = bf16[896,2560]{1,0:T(8,128)(2,1)} custom-call(bf16[896,4096]{1,0:T(8,128)(2,1)} %get-tuple-element.55.at_ref, bf16[4096,1280]{1,0:T(8,128)(2,1)} %get-tuple-element.58.refs_0_.dgb_ref, bf16[4096,1280]{1,0:T(8,128)(2,1)} %get-tuple-element.59.refs_1_.dub_ref), custom_call_target="tpu_custom_call" | custom-call | flops 18790481920 | bytes 32899072 | tf_op jit(solution)/shard_map/gradient/pallas_call | solution.py:377
  283.6 27.1 %gradient.7 = bf16[2560,896]{1,0:T(8,128)(2,1)} custom-call(bf16[896,4096]{1,0:T(8,128)(2,1)} %get-tuple-element.61.at_ref, bf16[4096,1280]{1,0:T(8,128)(2,1)} %get-tuple-element.62.refs_0_, bf16[4096,1280]{1,0:T(8,128)(2,1)} %get-tuple-element.63.refs_1_), custom_call_target="tpu_custom_call" | custom-call | flops 18790481920 | bytes 32899072 | tf_op jit(solution)/shard_map/gradient/pallas_call | solution.py:377
  310.9 53.7 %states.1 = (bf16[4096,896]{1,0:T(8,128)(2,1)}, bf16[896,4096]{1,0:T(8,128)(2,1)}) custom-call(bf16[4096,1280]{1,0:T(8,128)(2,1)} %get-tuple-element.54.refs_0_.dga_ref, bf16[4096,1280]{1,0:T(8,128)(2,1)} %get-tuple-element.58.refs_0_.dgb_ref, bf16[4096,1280]{1,0:T(8,128)(2,1)} %get-tuple-element.56.refs_1_.dua_ref, ...), custom_call_target="tpu_custom_call" | custom-call | flops 37580963840 | bytes 80478208 | tf_op jit(solution)/shard_map/states/pallas_call | solution.py:500
  364.6 26.1 %gradient.8 = bf16[2560,896]{1,0:T(8,128)(2,1)} custom-call(bf16[896,4096]{1,0:T(8,128)(2,1)} %get-tuple-element.66.at_ref, bf16[4096,2560]{1,0:T(8,128)(2,1)} %get-tuple-element.48.act_ref.refs_0_), custom_call_target="tpu_custom_call" | custom-call | flops 18790481920 | bytes 32899072 | tf_op jit(solution)/shard_map/gradient/pallas_call | solution.py:377
  390.8 27.2 %kept_hidden.2 = (bf16[4096,1024]{1,0:T(8,128)(2,1)}, bf16[4096,1024]{1,0:T(8,128)(2,1)}) custom-call(f32[4096,1024]{1,0:T(8,128)} %get-tuple-element.46.gate_ref, f32[4096,1024]{1,0:T(8,128)} %get-tuple-element.47.up_ref, bf16[4096,896]{1,0:T(8,128)(2,1)} %get-tuple-element.73.dy_ref, bf16[2560,896]{1,0:T(8,128)(2,1)} %get-tuple-element.49.wd_ref), custom_call_target="tpu_custom_call" | custom-call | flops 7516192768 | bytes 59506688 | tf_op jit(solution)/shard_map/kept_hidden/pallas_call | solution.py:339
  418.0 22.1 %gradient.9 = bf16[896,2048]{1,0:T(8,128)(2,1)} custom-call(bf16[896,4096]{1,0:T(8,128)(2,1)} %get-tuple-element.70.at_ref, bf16[4096,1024]{1,0:T(8,128)(2,1)} %get-tuple-element.68.refs_0_, bf16[4096,1024]{1,0:T(8,128)(2,1)} %get-tuple-element.69.refs_1_), custom_call_target="tpu_custom_call" | custom-call | flops 15032385536 | bytes 27787264 | tf_op jit(solution)/shard_map/gradient/pallas_call | solution.py:377
  440.2 0.1 fusion.17
  440.2 1.1 copy-done.4
  441.3 0.1 fusion.16
  441.4 1.1 maximum_bitcast_fusion.1
  442.5 1.1 maximum_bitcast_fusion.3
  443.6 36.1 %kept_hidden.3 = (bf16[4096,1536]{1,0:T(8,128)(2,1)}, bf16[4096,1536]{1,0:T(8,128)(2,1)}) custom-call(f32[4096,1536]{1,0:T(8,128)} %get-tuple-element.71.gate_ref, f32[4096,1536]{1,0:T(8,128)} %get-tuple-element.72.up_ref, bf16[4096,896]{1,0:T(8,128)(2,1)} %get-tuple-element.73.dy_ref, bf16[2560,896]{1,0:T(8,128)(2,1)} %get-tuple-element.49.wd_ref), custom_call_target="tpu_custom_call" | custom-call | flops 11274289152 | bytes 85590016 | tf_op jit(solution)/shard_map/kept_hidden/pallas_call | solution.py:339
  479.6 66.9 %last_gradient.1.refs_5_ = bf16[224,3072]{1,0:T(8,128)(2,1)} custom-call(bf16[896,4096]{1,0:T(8,128)(2,1)} %get-tuple-element.70.at_ref, bf16[4096,1536]{1,0:T(8,128)(2,1)} %get-tuple-element.74.refs_0_, bf16[4096,1536]{1,0:T(8,128)(2,1)} %get-tuple-element.75.refs_1_), custom_call_target="tpu_custom_call" | custom-call | flops 45097156608 | bytes 38010880 | tf_op jit(solution)/shard_map/last_gradient/pallas_call | solution.py:463
  546.5 2.4 fusion.15
  548.9 1.2 fusion.18
  550.2 1.2 copy-done.2
  551.4 1.3 copy-done.5
  552.7 1.3 copy-done.7
  554.0 1.2 copy-done.8
  555.1 7.8 %clip_factor.1 = f32[8,128]{1,0:T(8,128)S(1)} custom-call(bf16[224,2560]{1,0:T(8,128)(2,1)S(1)} %copy-done.5, bf16[224,2560]{1,0:T(8,128)(2,1)S(1)} %copy-done.7, bf16[640,896]{1,0:T(8,128)(2,1)S(1)} %copy-done.1, bf16[640,896]{1,0:T(8,128)(2,1)S(1)} %copy-done.2, bf16[224,2048]{1,0:T(8,128)(2,1)S(1)} %copy-done.8, bf16[224,3072]{1,0:T(8,128)(2,1)S(1)} %copy-done), custom_call_target="tpu_custom_call" | custom-call | flops 27525120 | bytes 6881280 | tf_op jit(solution)/shard_map/clip_factor/pallas_call | solution.py:547
  563.0 0.6 slice.3
  563.6 0.1 maximum_bitcast_fusion
  563.7 0.1 maximum_bitcast_fusion.2
  563.8 9.1 %fusion.8 = (bf16[2,640,896]{2,1,0:T(8,128)(2,1)}, f32[2,640,896]{2,1,0:T(8,128)}, f32[2,640,896]{2,1,0:T(8,128)}) fusion(bf16[2,640,896]{2,1,0:T(8,128)(2,1)S(1)} %copy-done.12, f32[]{:T(128)} %bitcast.4, bf16[1,640,896]{2,1,0:T(8,128)(2,1)S(1)} %bitcast.13, bf16[1,640,896]{2,1,0:T(8,128)(2,1)S(1)} %bitcast.14, f32[2,640,896]{2,1,0:T(8,128)} %param.21, ...), kind=kLoop, calls=%fused_computation.17 | loop fusion | flops 22937600 | bytes 25231364 | tf_op jit(solution)/shard_map/convert_element_type | solution.py:563
  572.9 15.3 %fusion.2 = (bf16[2,224,2560]{2,1,0:T(8,128)(2,1)}, f32[2,224,2560]{2,1,0:T(8,128)}, f32[2,224,2560]{2,1,0:T(8,128)}, bf16[2,224,2560]{2,1,0:T(8,128)(2,1)}, f32...) fusion(bf16[2,224,2560]{2,1,0:T(8,128)(2,1)} %refs_1_.3, f32[]{:T(128)} %bitcast.4, bf16[1,224,2560]{2,1,0:T(8,128)(2,1)S(1)} %copy-done.9, ...), kind=kLoop, calls=%fused_computation.11 | loop fusion | flops 45875200 | bytes 50462724 | tf_op jit(solution)/shard_map/convert_element_type | solution.py:563
  (35 shorter events, 0.6 us)
Async XLA Ops:
  7.2 303.7 %reduce-scatter.6.cloned.1.call-start = ((), (), s32[]{:S(2)}) async-start(), calls=%async_computation.5 | async-start | bytes 5734400 | tf_op jit(solution)/shard_map/reduce_scatter | solution.py:570
  215.3 175.5 %reduce-scatter.8.cloned.1.call-start = ((), (), s32[]{:S(2)}) async-start(), calls=%async_computation.6 | async-start | bytes 5734400 | tf_op jit(solution)/shard_map/reduce_scatter | solution.py:570
  283.5 156.6 %reduce-scatter.14.cloned.1.call-start = ((), (), s32[]{:S(2)}) async-start(), calls=%async_computation.9 | async-start | bytes 5734400 | tf_op jit(solution)/shard_map/reduce_scatter | solution.py:570
  310.8 168.9 %reduce-scatter.12.cloned.1.call-start = ((), (), s32[]{:S(2)}) async-start(), calls=%async_computation.8 | async-start | bytes 5734400 | tf_op jit(solution)/shard_map/reduce_scatter | solution.py:570
  390.7 158.2 %reduce-scatter.10.cloned.1.call-start = ((), (), s32[]{:S(2)}) async-start(), calls=%async_computation.7 | async-start | bytes 4587520 | tf_op jit(solution)/shard_map/reduce_scatter | solution.py:570
  418.0 22.2 %copy-start.6 = (bf16[224,2560]{1,0:T(8,128)(2,1)S(1)}, bf16[224,2560]{1,0:T(8,128)(2,1)}, u32[]{:S(2)}) copy-start(bf16[224,2560]{1,0:T(8,128)(2,1)} %reduce-scatter.8.cloned.1.call-done.refs_1_) | copy-start | bytes 3440644
  440.1 1.3 copy-start.4
  546.5 3.6 copy-start
  546.5 3.6 copy-start.1
  550.2 1.3 copy-start.2
  551.4 1.3 copy-start.5
  552.7 1.3 copy-start.7
  554.0 1.2 copy-start.8
  555.1 8.5 %copy-start.11 = (bf16[224,1536]{1,0:T(8,128)(2,1)S(1)}, bf16[224,1536]{1,0:T(8,128)(2,1)}, u32[]{:S(2)}) copy-start(bf16[224,1536]{1,0:T(8,128)(2,1)} %get-tuple-element.86) | copy-start | bytes 2064388
  555.1 8.6 %copy-start.3 = (bf16[640,896]{1,0:T(8,128)(2,1)S(1)}, bf16[640,896]{1,0:T(8,128)(2,1)}, u32[]{:S(2)}) copy-start(bf16[640,896]{1,0:T(8,128)(2,1)} %reduce-scatter.12.cloned.1.call-done.refs_3_) | copy-start | bytes 3440644
  555.1 8.6 %copy-start.12 = (bf16[2,640,896]{2,1,0:T(8,128)(2,1)S(1)}, bf16[2,640,896]{2,1,0:T(8,128)(2,1)}, u32[]{:S(2)}) copy-start(bf16[2,640,896]{2,1,0:T(8,128)(2,1)} %refs_0_.5) | copy-start | bytes 6881284
  563.8 9.1 %copy-start.9 = (bf16[1,224,2560]{2,1,0:T(8,128)(2,1)S(1)}, bf16[1,224,2560]{2,1,0:T(8,128)(2,1)}, u32[]{:S(2)}) copy-start(bf16[1,224,2560]{2,1,0:T(8,128)(2,1)} %maximum_bitcast_fusion.1) | copy-start | bytes 3440644
  563.8 9.1 %copy-start.10 = (bf16[1,224,2560]{2,1,0:T(8,128)(2,1)S(1)}, bf16[1,224,2560]{2,1,0:T(8,128)(2,1)}, u32[]{:S(2)}) copy-start(bf16[1,224,2560]{2,1,0:T(8,128)(2,1)} %maximum_bitcast_fusion.3) | copy-start | bytes 3440644
Sparse Core Ops, SparseCore 0:
  215.4 45.4 reduce-scatter.5
  283.6 45.4 reduce-scatter.7
  332.0 45.6 reduce-scatter.13
  390.8 45.4 reduce-scatter.11
  440.2 37.9 reduce-scatter.9
